TPU v7x, 256 devices: a whole 4x4x8 slice. The times are simulated.
256 devices in a mesh: gx: 32 (over x, z), gy: 4 (over y), gz: 2 (over core).
Axes of the slice: x: 4, y: 4, z: 8, core: 2. Of those that a mesh axis runs over, the one named last changes fastest.
Arguments:
- coarse_field: float32 [3, 1024, 128, 512], P(None, 'gx', 'gy', 'gz'), may hold values from -6 to 6
- fine_field: float32 [3, 1024, 16, 256], P(None, ('gx', 'gy', 'gz')), may hold values from -6 to 6
- viscosity: float32 [1024, 16, 256], P(('gx', 'gy', 'gz')), may hold values from 0.1 to 1
- corners: int32 [512, 3], replicated, may hold values from 0 to 1016, as said below
- grid_slot: int32 [512], replicated, may hold values from 0 to 1023, as said below
- neighbors: int32 [512, 2], replicated, may hold values from -1 to 511, as said below
Outputs:
- fine_out: float32 [3, 1024, 16, 256], P(None, ('gx', 'gy', 'gz'))
- coarse_out: float32 [3, 1024, 128, 512], P(None, 'gx', 'gy', 'gz')
Inputs may be any that keep to these rules, and one draw needn't show every extreme that they name: Each box is 8 coarse cells on a side, its corner coordinates are multiples of 8, it lies inside the domain and inside one coarse brick of 32 x 32 x 256 cells, and different grids have different boxes. A brick holds either no box or exactly 4 boxes, which share their y and z corners and are grids of one wake. `grid_slot`: different grids have different slots. A grid's slot lies on a device with the same gz index as the brick that holds its box. Every device holds at most 4 grids, some device holds 4 grids in every draw, and all grids of one device lie in one brick. `neighbors`: entry 0 is the grid of the same wake whose box touches the grid's lower x face, entry 1 the one touching its upper x face, or -1 where there is none.
All inputs are finite; a program needn't handle non-finite values.
Results may differ from a plain program's by a relative error of at most 0.00005.
Values sent between devices are 32-bit elements; how exact they have to be, the bound alone decides.
No kernel may reach another device: no remote copies, remote signals or barrier semaphores. Data moves between devices by JAX's collectives and lax.ppermute only.
A program may use at most 128 MiB of HBM per device.

v0:
```python
import functools

import jax
import jax.numpy as jnp
import numpy as np
from jax import lax
from jax.experimental import pallas as pl
from jax.experimental.pallas import tpu as pltpu
from jax.sharding import Mesh
from jax.sharding import PartitionSpec as P

B = 8
F = 16
SLOTS = 4
SIDE = B + 2
LINE_X = 4
LINE_Z = 8
LINE_Y = 4
PLANE = LINE_X * LINE_Y
HALO = 48
SEND = 72
HIGHEST = lax.Precision.HIGHEST
step_rate = 0.15
f32 = jnp.float32
i32 = jnp.int32
GX = ("gx_0", "gx_1")
GX_GY_GZ = ("gx_0", "gx_1", "gy", "gz")

ROW_SLOT, ROW_HOME, ROW_LOW, ROW_HIGH, ROW_OWNER, ROW_ANCHOR, ROW_ROUTE, ROW_SENDS = range(8)
SELF_TARGET = 8


def tangent_matrix():
    fine = np.arange(F)
    coarse = np.arange(SIDE)
    center = fine // 2 + 1
    other = np.where(fine % 2 == 0, center - 1, center + 1)
    return 0.75 * (coarse[None] == center[:, None]) + 0.25 * (coarse[None] == other[:, None])


def constant_matrices():
    tangent = tangent_matrix()
    along_x = np.zeros((64, 40))
    for fine in range(64):
        center = fine // 2
        other = center - 1 if fine % 2 == 0 else center + 1
        along_x[fine, center] += 0.75
        along_x[fine, 32 if other < 0 else 33 if other > 31 else other] += 0.25
    faces = np.zeros((128, 3, F, F))
    for k in range(3):
        for c in range(SIDE):
            faces[k * 10 + c, k, 0, :] += tangent[:, c]
            faces[30 + k * 10 + c, k, F - 1, :] += tangent[:, c]
            faces[60 + k * 10 + c, k, :, 0] += tangent[:, c]
            faces[90 + k * 10 + c, k, :, F - 1] += tangent[:, c]
    ends = np.zeros((128, F * F))
    ends[: SIDE * SIDE] = np.einsum("sa,tb->abst", tangent, tangent).reshape(SIDE * SIDE, F * F)
    pool = np.zeros((2, F, F, 128))
    for y in range(F):
        for z in range(F):
            for half in range(2):
                pool[half, y, z, half * 64 + (y // 2) * B + z // 2] = 0.125
    return (
        along_x.astype(np.float32),
        faces.reshape(128, 3 * F * F).astype(np.float32),
        ends.astype(np.float32),
        pool.reshape(2, F * F, 128).astype(np.float32),
    )


def pack_constants():
    out = np.zeros((40, 128))
    for k in range(3):
        for y in range(B):
            out[k * B + y, 60 + 10 * k + 1 + y] = 1.0
            out[k * B + y, 90 + 10 * k + 1 + y] = 1.0
        out[k * B, 10 * k : 10 * k + 10] = 0.25
        out[k * B + B - 1, 30 + 10 * k : 40 + 10 * k] = 0.25
        out[24 + k, 10 * k : 10 * k + 10] = 0.75
        out[24 + k, [60 + 10 * k, 90 + 10 * k]] = 1.0
        out[27 + k, 30 + 10 * k : 40 + 10 * k] = 0.75
        out[27 + k, [69 + 10 * k, 99 + 10 * k]] = 1.0
    lanes = np.arange(128)
    out[32] = np.where(lanes < 60, lanes % 10, np.where(lanes < 90, 0, np.where(lanes < 120, 9, -999)))
    out[33] = np.where(lanes < 60, -999, np.where(lanes < 90, 1, np.where(lanes < 120, 8, -999)))
    out[34] = np.where(lanes < 60, 1.0, 0.75)
    out[35] = 0.25
    return out.astype(np.float32)


def position():
    return tuple(lax.axis_index(name) for name in GX_GY_GZ)


def make_table(corners_ref, slots_ref, near_ref, table_ref):
    my_x, my_z, my_y, my_c = position()
    cx, cy, cz = corners_ref[0:1, :], corners_ref[1:2, :], corners_ref[2:3, :]
    gs = slots_ref[0:1, :]
    grids = gs.shape[1]
    low, high = near_ref[0:1, :], near_ref[1:2, :]
    gx, gy, gz = cx >> 5, cy >> 5, cz >> 8
    box = (cx >> 3) & 3
    home = gx * LINE_Y + gy
    brick_key = (home * 2 + gz) * SLOTS + box
    word = (1 + box * 2 + home * 8 + (low + 1) * 1024).astype(f32)
    sub = lax.broadcasted_iota(i32, (64, 1), 0)
    eye = (lax.broadcasted_iota(i32, (64, 128), 0) == lax.broadcasted_iota(i32, (64, 128), 1)).astype(f32)

    def to_row(column):
        return jnp.sum(eye * column, axis=0, keepdims=True)

    def pick(match, values):
        return jnp.sum(jnp.where(match, values, 0.0), axis=1, keepdims=True)

    def device_of(j):
        return (((j >> 2) * LINE_Z + my_z) * LINE_Y + (j & 3)) * 2 + my_c

    keys = device_of(sub >> 2) * SLOTS + (sub & 3)
    held = keys == gs
    words = pick(held, word)
    high_grid = pick(held, (high + 1).astype(f32)).astype(i32)
    low_grid = words.astype(i32) >> 10
    grid_ids = lax.broadcasted_iota(i32, (1, grids), 1) + 1
    slot_plus = (gs + 1).astype(f32)
    low_slot = pick(low_grid == grid_ids, slot_plus).astype(i32)
    high_slot = pick(high_grid == grid_ids, slot_plus).astype(i32)
    devices = gs >> 2
    bit = (jnp.int32(1) << box).astype(f32)

    def boxes_on(device):
        return pick(device == devices, bit).astype(i32)

    mine = device_of(sub >> 2)
    my_mask = boxes_on(mine)
    my_box = (words.astype(i32) >> 1) & 3
    lanes = lax.broadcasted_iota(i32, (64, 128), 1)
    same_j = (sub >> 2) == (lanes >> 2)
    route_row = jnp.zeros((1, 128), f32)
    sends_row = jnp.zeros((1, 128), f32)
    near_words = []
    for side, slot in enumerate((low_slot, high_slot)):
        device = (slot - 1) >> 2
        near_mask = boxes_on(device)
        near_box = (my_box + (3, 1)[side]) & 3
        outer = (slot > 0) & (device != mine)

        def before(mask, at):
            return ((mask & ((jnp.int32(1) << at) - 1)) != 0).astype(i32)

        def after(mask, at):
            return ((mask >> (at + 1)) != 0).astype(i32)

        if side == 0:
            here, there = before(my_mask, my_box), 2 + after(near_mask, near_box)
        else:
            here, there = 2 + after(my_mask, my_box), before(near_mask, near_box)
        target = jnp.where(same_j & ((lanes & 3) == here) & outer, 1.0, 0.0)
        code = (((device >> 3) & 7) * 4 + there + 1).astype(f32)
        route_row = route_row + jnp.sum(target * code, axis=0, keepdims=True)
        sends_row = sends_row + jnp.sum(target * ((sub & 3) + 1).astype(f32), axis=0, keepdims=True)
        plane = (device >> 6) * LINE_Y + ((device >> 1) & 3)
        word = jnp.where(outer, 2 + here * 4 + plane * 16, 1 + ((slot - 1) & 3) * 4)
        near_words.append(jnp.where(slot > 0, word, 0).astype(f32))
    owner = pick(keys == brick_key, slot_plus)
    sub16 = lax.broadcasted_iota(i32, (16, 1), 0)
    on_device = device_of(sub16) == (gs >> 2)
    homes = jnp.max(jnp.where(on_device, (home + 1).astype(f32), 0.0), axis=1, keepdims=True)
    homes = jnp.concatenate([homes, jnp.zeros((48, 1), f32)], axis=0)
    sub24 = lax.broadcasted_iota(i32, (24, 1), 0)
    target_x = my_x * LINE_Z + my_z + jnp.where(sub24 >= 12, 1, jnp.where(sub24 >= 6, 0, -1))
    target_x = jnp.where(sub24 >= 18, -1, target_x)
    in_x = sub24 - jnp.where(sub24 >= 12, 12, jnp.where(sub24 >= 6, 6, 0))
    target_y = my_y + (in_x >> 1) - 1
    target_z = jnp.where((in_x & 1) == 0, my_c, 1 - my_c)
    near_brick = (target_x == gx) & (target_y == gy) & (target_z == gz)
    place = ((cy & 31) * 256 + (cz & 255)).astype(f32)
    anchors = jnp.max(jnp.where(near_brick, place, -1.0), axis=1, keepdims=True)
    anchors = jnp.concatenate([anchors, jnp.zeros((40, 1), f32)], axis=0)
    rows = [to_row(v) for v in (words, homes, *near_words, owner, anchors)] + [route_row, sends_row]
    for r, row in enumerate(rows):
        table_ref[r : r + 1, :] = row.astype(i32)


def pack_kernel(
    corners_ref, slots_ref, near_ref, fine_ref, brick, const,
    table_ref, own_ref, other_ref, planes_ref,
    table, table_sem,
):
    make_table(corners_ref, slots_ref, near_ref, table_ref)
    fetch = pltpu.make_async_copy(table_ref, table, table_sem)
    fetch.start()
    own_ref[...] = jnp.zeros_like(own_ref)
    other_ref[...] = jnp.zeros_like(other_ref)
    planes_ref[...] = jnp.zeros_like(planes_ref)
    fetch.wait()
    me = lax.axis_index("gx_0") * LINE_Y + lax.axis_index("gy")
    for e in range(4):
        s = jnp.maximum(table[ROW_SENDS, me * 4 + e] - 1, 0)
        for k in range(3):
            tile = fine_ref[pl.ds(pl.multiple_of((k * SLOTS + s) * F + (0 if e < 2 else 8), 8), 8), :]
            row = tile[0:1] if e < 2 else tile[7:8]
            for half in range(2):
                at = e * 8 + half * 3 + k
                planes_ref[at : at + 1, :] = row[:, half * 128 : half * 128 + 128]

    my_c = lax.axis_index("gz")
    lane = lax.broadcasted_iota(i32, (1, 128), 1)
    sub3 = lax.broadcasted_iota(i32, (3, 1), 0)

    def shifted(start, count, stride, z_base, valid):
        rows = jnp.concatenate(
            [brick[pl.ds(start + 8 * half, count, stride=stride), :] for half in range(2)], axis=1
        )
        rows = pltpu.roll(rows, (256 - z_base) & 255, 1)[:, :128]
        at = z_base + lane
        keep = (lane < SIDE) & (at >= 0) & (at < 256) & valid
        return jnp.where(keep, rows, 0.0)

    def tile_row(y):
        return (y >> 3) * 16 + (y & 7)

    def layers(dy, y0):
        if dy == 0:
            for t in range(SIDE):
                y = y0 - 1 + t
                valid = True if 0 < t < SIDE - 1 else (y >= 0) & (y < 32)
                yield t, jnp.clip(y, 0, 31), valid
        elif dy == 1:
            yield 0, 31, y0 == 0
        else:
            yield SIDE - 1, 0, y0 == 24

    weights = {0: (0.75, 0), 1: (0.25, 0), SIDE - 2: (0.25, 30), SIDE - 1: (0.75, 30)}

    def ends_of(u):
        low = 0.75 * u[:, 0:1] + 0.25 * u[:, 1:2]
        high = 0.75 * u[:, 9:10] + 0.25 * u[:, 8:9]
        return low, high

    def main_rows(dy, y0, z_base):
        total = jnp.zeros((32, 128), f32)
        for t, y, valid in layers(dy, y0):
            for k in range(3):
                u = shifted(k * 2048 + tile_row(y), 32, 64, z_base, valid)
                low, high = ends_of(u)
                total = jnp.where(lane == 60 + 10 * k + t, low, total)
                total = jnp.where(lane == 90 + 10 * k + t, high, total)
                if t in weights:
                    w, face = weights[t]
                    total = total + w * (pltpu.roll(u, face + 10 * k, 1) if face + k else u)
        return total

    def all_rows(y0, z_base):
        offset = lax.broadcasted_iota(i32, (256, 1), 0) - z_base
        offset = offset.astype(f32)
        window = jnp.where(offset == const[32:33, :], const[34:35, :], 0.0)
        window = window + jnp.where(offset == const[33:34, :], const[35:36, :], 0.0)
        start = (y0 >> 3) * 16
        low_y, high_y = jnp.maximum(y0 - 1, 0), jnp.minimum(y0 + B, 31)
        sides = []
        for half in range(2):
            parts = [brick[pl.ds(pl.multiple_of(n * 64 + start + half * 8, 8), 8), :] for n in range(96)]
            for y in (low_y, high_y):
                parts.append(brick[pl.ds(tile_row(y) + half * 8, 96, stride=64), :])
            sides.append(jnp.concatenate(parts, axis=0))
        cells = jnp.dot(
            jnp.concatenate(sides, axis=1), window, precision=HIGHEST, preferred_element_type=f32
        )
        inner = cells[:768].reshape(3, 32, B, 128)
        total = inner[0] * const[0:8, :][None]
        total = total + inner[1] * const[8:16, :][None]
        total = total + inner[2] * const[16:24, :][None]
        rows = jnp.sum(total, axis=1)
        for k in range(3):
            low = jnp.where(y0 > 0, const[24 + k : 25 + k, :], 0.0)
            high = jnp.where(y0 < 24, const[27 + k : 28 + k, :], 0.0)
            rows = rows + low * cells[768 + 32 * k : 800 + 32 * k] + high * cells[864 + 32 * k : 896 + 32 * k]
        return rows

    def edge_rows(x, dy, y0, z_base, with_row):
        flat = jnp.zeros((3, 128), f32)
        row = jnp.zeros((3, 128), f32)
        for t, y, valid in layers(dy, y0):
            u = shifted(x * 64 + tile_row(y), 3, 2048, z_base, valid)
            flat = flat + (pltpu.roll(u, 10 * t, 1) if t else u)
            if with_row:
                low, high = ends_of(u)
                row = jnp.where(lane == 60 + 10 * sub3 + t, low, row)
                row = jnp.where(lane == 90 + 10 * sub3 + t, high, row)
                if t in weights:
                    w, face = weights[t]
                    spread = jnp.where(
                        sub3 == 0,
                        pltpu.roll(u, face, 1) if face else u,
                        jnp.where(sub3 == 1, pltpu.roll(u, face + 10, 1), pltpu.roll(u, face + 20, 1)),
                    )
                    row = row + w * spread
        return flat, jnp.sum(row, axis=0, keepdims=True)

    for dz in range(2):
        out = other_ref if dz else own_ref
        z_shift = 256 * (1 - 2 * my_c) if dz else 0
        for dy in (-1, 0, 1):
            base = (dy + 1) * HALO
            for dx in (0, -1, 1):
                place = table[ROW_ANCHOR, (dx + 1) * 6 + (dy + 1) * 2 + dz]
                y0, z0 = place >> 8, place & 255
                z_base = z0 - 1 + z_shift
                near = place >= 0
                if dy == 1:
                    near &= y0 == 0
                if dy == -1:
                    near &= y0 == 24
                if dz:
                    near &= z0 == jnp.where(my_c == 0, 0, 248)

                @pl.when(near)
                def _(out=out, base=base, dx=dx, dy=dy, y0=y0, z_base=z_base):
                    if dx == 0:
                        out[base : base + 32, :] = main_rows(dy, y0, z_base) if dy else all_rows(y0, z_base)
                        for x, at in ((0, 0), (31, 3)):
                            flat, _row = edge_rows(x, dy, y0, z_base, False)
                            out[base + 32 + at : base + 35 + at, :] = 0.25 * flat
                    else:
                        x, at = (0, base + 44) if dx == -1 else (31, base + 40)
                        flat, row = edge_rows(x, dy, y0, z_base, True)
                        out[at : at + 3, :] = 0.75 * flat
                        out[at + 3 : at + 4, :] = row


def split_slot(slot):
    device = slot >> 2
    return device >> 6, (device >> 3) & 7, (device >> 1) & 3, slot & 3


def join_kernel(middle, above, below, planes, out):
    total = middle[...] + above[...] + below[...]
    sub = lax.broadcasted_iota(i32, (8, 1), 0)
    tiles = []
    for e in range(4):
        pair = jnp.where(sub == 6, total[40 + 2 * e : 41 + 2 * e], total[41 + 2 * e : 42 + 2 * e])
        tiles.append(jnp.where(sub < 6, planes[e * 8 : e * 8 + 8, :], pair))
    payload = jnp.concatenate([total[:40]] + tiles, axis=0)
    for z in range(LINE_Z):
        out[z] = payload


def route_kernel(table, held, out):
    sub = lax.broadcasted_iota(i32, (8, 1), 0)
    for j in range(PLANE):
        home = jnp.maximum(table[ROW_HOME, j] - 1, 0)
        z = (home >> 2) & 7
        out[j, 0:40] = held[z, 0:40]
        for e in range(4):
            code = jnp.maximum(table[ROW_ROUTE, j * 4 + e] - 1, 0)
            start = pl.multiple_of(40 + (code & 3) * 8, 8)
            at = 40 + e * 8
            piece = held[(z + (7 if e < 2 else 1)) & 7, at : at + 8]
            out[j, at : at + 8] = jnp.where(sub < 6, held[code >> 2, pl.ds(start, 8)], piece)


def update_kernel(
    table, rcv, fine_ref, visc_ref, along_x, faces, ends, pool,
    fine_out, means_out,
    sums, planes, advanced, pooled,
):
    my_x, _, my_y, _ = position()
    me = my_x * LINE_Y + my_y
    home = jnp.maximum(table[ROW_HOME, me] - 1, 0)
    gx, hy = home >> 2, home & 3
    at_home = (gx >> 3) * LINE_Y + hy
    at_low = (jnp.maximum(gx - 1, 0) >> 3) * LINE_Y + hy
    at_high = (jnp.minimum(gx + 1, 31) >> 3) * LINE_Y + hy
    sub8 = lax.broadcasted_iota(i32, (8, 1), 0)

    def piece_rows(at, tile, inside):
        pair = [jnp.where(inside, rcv[at, tile + 8 * i : tile + 8 * i + 8], 0.0) for i in range(2)]
        return pair[0][6:7], pair[0][7:8], pair[1][6:7], pair[1][7:8]

    low = piece_rows(at_low, 40, gx > 0)
    high = piece_rows(at_high, 56, gx < 31)
    beyond = jnp.where(sub8 == 0, low[3], jnp.where(sub8 == 1, high[3], 0.0))
    body = jnp.concatenate([rcv[at_home, 0:32], beyond], axis=0)
    dot = functools.partial(jnp.dot, precision=HIGHEST, preferred_element_type=f32)
    sums[...] = dot(dot(along_x[...], body), faces[...])
    flat = rcv[at_home, 32:40]
    for i, row in enumerate(low[:3] + high[:3]):
        flat = flat + jnp.where(sub8 == i, row, 0.0)
    planes[...] = dot(flat, ends[...])
    lane = lax.broadcasted_iota(i32, (1, F * F), 1)
    sub = lax.broadcasted_iota(i32, (F, 1), 0)
    lane_z = lane & (F - 1)
    for s in range(SLOTS):
        word = table[ROW_SLOT, me * 4 + s]
        active = (word & 1) == 1
        box_start = pl.multiple_of(((word >> 1) & 3) * F, F)
        low_word = table[ROW_LOW, me * 4 + s]
        high_word = table[ROW_HIGH, me * 4 + s]
        low_tile = rcv[low_word >> 4, pl.ds(pl.multiple_of(40 + ((low_word >> 2) & 3) * 8, 8), 8)]
        high_tile = rcv[high_word >> 4, pl.ds(pl.multiple_of(40 + ((high_word >> 2) & 3) * 8, 8), 8)]
        visc = step_rate * visc_ref[s * F : s * F + F, :]
        for k in range(3):
            row = (k * SLOTS + s) * F
            cells = fine_ref[row : row + F, :]
            lower = jnp.concatenate([low_tile[k : k + 1], low_tile[3 + k : 4 + k]], axis=1)
            upper = jnp.concatenate([high_tile[k : k + 1], high_tile[3 + k : 4 + k]], axis=1)
            low_row = pl.multiple_of((k * SLOTS + ((low_word >> 2) & 3)) * F + 8, 8)
            high_row = pl.multiple_of((k * SLOTS + ((high_word >> 2) & 3)) * F, 8)
            lower = jnp.where((low_word & 3) == 1, fine_ref[pl.ds(low_row, 8), :][7:8], lower)
            upper = jnp.where((high_word & 3) == 1, fine_ref[pl.ds(high_row, 8), :][0:1], upper)
            lower = jnp.where(low_word > 0, lower, planes[k : k + 1, :])
            upper = jnp.where(high_word > 0, upper, planes[3 + k : 4 + k, :])
            total = sums[pl.ds(box_start, F), k * 256 : k * 256 + 256] - 6.0 * cells
            total = total + jnp.where(sub == 0, lower, pltpu.roll(cells, 1, 0))
            total = total + jnp.where(sub == F - 1, upper, pltpu.roll(cells, F - 1, 0))
            total = total + jnp.where(lane < F, 0.0, pltpu.roll(cells, F, 1))
            total = total + jnp.where(lane >= F * F - F, 0.0, pltpu.roll(cells, F * F - F, 1))
            total = total + jnp.where(lane_z == 0, 0.0, pltpu.roll(cells, 1, 1))
            total = total + jnp.where(lane_z == F - 1, 0.0, pltpu.roll(cells, F * F - 1, 1))
            result = cells + visc * total
            fine_out[row : row + F, :] = jnp.where(active, result, 0.0)
            at = s * 48 + k * F
            advanced[at : at + F, :] = result
    for p in range(2):
        at = p * 96
        pooled[p * 48 : p * 48 + 48, :] = dot(advanced[at : at + 48, :], pool[0]) + dot(
            advanced[at + 48 : at + 96, :], pool[1]
        )
    means = pooled[pl.ds(0, 48, stride=2), :] + pooled[pl.ds(1, 48, stride=2), :]
    for z in range(LINE_Z):
        means_out[z] = means


def return_kernel(table, held, out):
    first = lax.broadcasted_iota(i32, (1, 128), 1) < 64
    for j in range(PLANE):
        for p in range(2):
            picks = []
            for h in range(2):
                _, z, _, local = split_slot(jnp.maximum(table[ROW_OWNER, j * 4 + 2 * p + h] - 1, 0))
                start = pl.multiple_of((local >> 1) * 24, 8)
                rows = held[z, pl.ds(start, 24)]
                picks.append(jnp.where((local & 1) == h, rows, pltpu.roll(rows, 64, 1)))
            out[j, p * 24 : p * 24 + 24] = jnp.where(first, picks[0], picks[1])


def place_kernel(table, rcv, coarse_ref, coarse_out, window, spread, sem):
    my_x, _, my_y, _ = position()
    me = my_x * LINE_Y + my_y
    place = table[ROW_ANCHOR, SELF_TARGET]

    @pl.when(place >= 0)
    def _():
        y0 = pl.multiple_of(place >> 8, 8)
        z0 = place & 255
        z_tile = pl.multiple_of((z0 >> 7) * 128, 128)
        z_in = z0 & 127
        region = coarse_out.at[:, pl.ds(y0, 8), pl.ds(z_tile, 128)]
        load = pltpu.make_async_copy(region, window, sem.at[0])
        load.start()
        for i in range(SLOTS):
            ox, _, oy, _ = split_slot(jnp.maximum(table[ROW_OWNER, me * 4 + i] - 1, 0))
            at = ox * LINE_Y + oy
            for k in range(3):
                start = ((i // 2) * 3 + k) * 8
                values = rcv[at, start : start + 8]
                for b in range(B):
                    shift = (z_in + 256 - (b * B + 64 * (i % 2))) & 127
                    spread[pl.ds((k * 32 + i * B) * B + b, B, stride=B), :] = pltpu.roll(values, shift, 1)
        load.wait()
        lane = lax.broadcasted_iota(i32, (1, 1, 128), 2)
        fresh = spread[...].reshape(96, 8, 128)
        window[...] = jnp.where((lane >= z_in) & (lane < z_in + B), fresh, window[...])
        store = pltpu.make_async_copy(window, region, sem.at[1])
        store.start()
        store.wait()


def vmem():
    return pl.BlockSpec(memory_space=pltpu.VMEM)


def smem():
    return pl.BlockSpec(memory_space=pltpu.SMEM)


def anywhere():
    return pl.BlockSpec(memory_space=pl.ANY)


def shape(*dims, dtype=f32):
    return jax.ShapeDtypeStruct(dims, dtype)


def on_device(coarse_field, fine_field, viscosity, corners, grid_slot, neighbors):
    fine = fine_field.reshape(3 * SLOTS * F, F * F)
    tiles = coarse_field.reshape(3, 32, 4, 8, 2, 128).transpose(0, 1, 2, 4, 3, 5).reshape(6144, 128)
    table, own, other, planes = pl.pallas_call(
        pack_kernel,
        out_shape=(
            shape(8, 128, dtype=i32),
            shape(3 * HALO, 128),
            shape(3 * HALO, 128),
            shape(32, 128),
        ),
        in_specs=[vmem()] * 6,
        out_specs=(vmem(), vmem(), vmem(), vmem()),
        scratch_shapes=[pltpu.SMEM((8, 128), i32), pltpu.SemaphoreType.DMA(())],
        name="pack", compiler_params=pltpu.CompilerParams(vmem_limit_bytes=24 << 20),
    )(corners.T, grid_slot[None, :], neighbors.T, fine, tiles, jnp.asarray(pack_constants()))
    halo = own + lax.ppermute(other, "gz", [(0, 1), (1, 0)])
    halo = halo.reshape(3, HALO, 128)
    above = lax.ppermute(halo[2], "gy", [(i, i + 1) for i in range(LINE_Y - 1)])
    below = lax.ppermute(halo[0], "gy", [(i + 1, i) for i in range(LINE_Y - 1)])
    payload = pl.pallas_call(
        join_kernel,
        out_shape=shape(LINE_Z, SEND, 128),
        in_specs=[vmem()] * 4,
        out_specs=vmem(),
        name="join",
        compiler_params=pltpu.CompilerParams(vmem_limit_bytes=8 << 20),
    )(halo[1], above, below, planes)
    held = lax.all_to_all(payload, "gx_1", 0, 0)
    routed = pl.pallas_call(
        route_kernel,
        out_shape=shape(PLANE, SEND, 128),
        in_specs=[smem(), vmem()],
        out_specs=vmem(),
        name="route", compiler_params=pltpu.CompilerParams(vmem_limit_bytes=8 << 20),
    )(table, held)
    received = lax.all_to_all(routed, ("gx_0", "gy"), 0, 0)
    fine_out, means = pl.pallas_call(
        update_kernel,
        out_shape=(shape(3 * SLOTS * F, F * F), shape(LINE_Z, 48, 128)),
        in_specs=[smem()] + [vmem()] * 7,
        out_specs=(vmem(), vmem()),
        scratch_shapes=[
            pltpu.VMEM((64, 768), f32),
            pltpu.VMEM((8, 256), f32),
            pltpu.VMEM((192, 256), f32),
            pltpu.VMEM((96, 128), f32),
        ],
        name="update", compiler_params=pltpu.CompilerParams(vmem_limit_bytes=16 << 20),
    )(table, received, fine, viscosity.reshape(SLOTS * F, F * F), *map(jnp.asarray, constant_matrices()))
    held_means = lax.all_to_all(means, "gx_1", 0, 0)
    back = pl.pallas_call(
        return_kernel,
        out_shape=shape(PLANE, 48, 128),
        in_specs=[smem(), vmem()],
        out_specs=vmem(),
        name="send_back", compiler_params=pltpu.CompilerParams(vmem_limit_bytes=8 << 20),
    )(table, held_means)
    returned = lax.all_to_all(back, ("gx_0", "gy"), 0, 0)
    coarse_out = pl.pallas_call(
        place_kernel,
        out_shape=shape(96, 32, 256),
        in_specs=[smem(), vmem(), anywhere()],
        out_specs=anywhere(),
        input_output_aliases={2: 0},
        scratch_shapes=[
            pltpu.VMEM((96, 8, 128), f32),
            pltpu.VMEM((768, 128), f32),
            pltpu.SemaphoreType.DMA((2,)),
        ],
        name="place", compiler_params=pltpu.CompilerParams(vmem_limit_bytes=8 << 20),
    )(table, returned, coarse_field.reshape(96, 32, 256))
    return fine_out.reshape(fine_field.shape), coarse_out.reshape(coarse_field.shape)


def solution(mesh):
    split = Mesh(
        mesh.devices.reshape(LINE_X, LINE_Z, mesh.shape["gy"], mesh.shape["gz"]), ("gx_0", "gx_1", "gy", "gz")
    )
    in_specs = (
        P(None, GX, "gy", "gz"),
        P(None, GX_GY_GZ, None, None),
        P(GX_GY_GZ, None, None),
        P(),
        P(),
        P(),
    )
    out_specs = (P(None, GX_GY_GZ, None, None), P(None, GX, "gy", "gz"))
    return jax.shard_map(
        on_device, mesh=split, in_specs=in_specs, out_specs=out_specs, check_vma=False
    )
```

profile of v0, /device:TPU:2, one launch (start us, length us, event | category | flops | bytes accessed | tf_op | source)
XLA Modules:
  0.0 81.7 jit_solution(11461600572499407420)
XLA Ops:
  0.6 0.0 copy-start.7
  0.6 0.0 copy-start.1
  0.7 0.0 copy-start.8
  0.7 0.0 copy-start.10
  0.7 0.0 copy-start.9
  0.7 2.0 %copy.16 = f32[3,32,32,256]{3,2,1,0:T(8,128)S(1)} copy(f32[3,32,32,256]{3,2,1,0:T(8,128)} %param.11) | data formatting | bytes 6291456
  2.6 0.0 copy-start
  2.6 0.0 copy-done.7
  2.6 0.0 copy-done.1
  2.6 0.0 copy-done.8
  2.7 0.0 copy-done.10
  2.7 0.0 copy-done.9
  2.7 0.0 copy-start.2
  2.7 0.0 copy-start.3
  2.7 0.0 copy-start.4
  2.7 0.0 copy-start.5
  2.7 0.0 copy-start.6
  2.7 2.8 %pack.1 = (s32[8,128]{1,0:T(8,128)S(1)}, f32[144,128]{1,0:T(8,128)S(1)}, f32[144,128]{1,0:T(8,128)S(1)}, f32[32,128]{1,0:T(8,128)S(1)}) custom-call(s32[3,512]{1,0:T(4,128)S(1)} %bitcast.19, s32[1,512]{1,0:T(1,128)S(1)} %bitcast.21, s32[2,512]{1,0:T(2,128)S(1)} %bitcast.20, f32[192,256]{1,0:T(8,128)S(1)} %bitcast.16, f32[6144,128]{1,0:T(8,128)S(1)} %bitcast.13, ...), custom_call_target="tpu_custom_call" | custom-call | tf_op jit(solution)/shard_map/pack/pallas_call | solution.py:498
  5.5 0.1 collective-permute-start
  5.6 1.3 %collective-permute-done = f32[144,128]{1,0:T(8,128)S(1)} collective-permute-done((f32[144,128]{1,0:T(8,128)S(1)}, f32[144,128]{1,0:T(8,128)S(1)}, u32[]{:S(2)}, u32[]{:S(2)}) %collective-permute-start) | collective-permute-done | bytes 73760 | tf_op jit(solution)/shard_map/ppermute | solution.py:511
  6.9 1.3 %collective-permute-start.2 = (f32[48,128]{1,0:T(8,128)S(1)}, f32[48,128]{1,0:T(8,128)S(1)}, u32[]{:S(2)}, u32[]{:S(2)}) collective-permute-start(f32[48,128]{1,0:T(8,128)S(1)} %get-tuple-element.14), channel_id=1, source_target_pairs={{2,0},{4,2},{6,4},{3,1},{5,3},{7,5},{10,8},{12,10},{14,12},{11,9},... | collective-permute-start | bytes 73736 | tf_op jit(solution)/shard_map/ppermute | solution.py:514
  8.2 4.5 %collective-permute-start.1 = (f32[48,128]{1,0:T(8,128)S(1)}, f32[48,128]{1,0:T(8,128)S(1)}, u32[]{:S(2)}, u32[]{:S(2)}) collective-permute-start(f32[48,128]{1,0:T(8,128)S(1)} %get-tuple-element.15), channel_id=1, source_target_pairs={{0,2},{2,4},{4,6},{1,3},{3,5},{5,7},{8,10},{10,12},{12,14},{9,11},... | collective-permute-start | bytes 73736 | tf_op jit(solution)/shard_map/ppermute | solution.py:513
  12.7 0.0 collective-permute-done.2.below
  12.7 1.5 %collective-permute-done.1.above = f32[48,128]{1,0:T(8,128)S(1)} collective-permute-done((f32[48,128]{1,0:T(8,128)S(1)}, f32[48,128]{1,0:T(8,128)S(1)}, u32[]{:S(2)}, u32[]{:S(2)}) %collective-permute-start.1) | collective-permute-done | bytes 24608 | tf_op jit(solution)/shard_map/ppermute | solution.py:513
  14.3 20.8 %all_to_all.20.held = f32[8,72,128]{2,1,0:T(8,128)S(1)} all-to-all(f32[8,72,128]{2,1,0:T(8,128)S(1)} %join.1), channel_id=1, replica_groups=mesh['gx_0'=4,'gx_1'=8,'gy'=4,'gz'=2] {'gx_1'}, dimensions={0} | all-to-all | bytes 589824 | tf_op jit(solution)/shard_map/all_to_all | solution.py:523
  35.0 0.8 %route.1 = f32[16,72,128]{2,1,0:T(8,128)S(1)} custom-call(s32[8,128]{1,0:T(8,128)S(1)} %get-tuple-element.8.table, f32[8,72,128]{2,1,0:T(8,128)S(1)} %all_to_all.20.held), custom_call_target="tpu_custom_call" | custom-call | tf_op jit(solution)/shard_map/route/pallas_call | solution.py:524
  35.9 16.1 %all_to_all.21.rcv = f32[16,72,128]{2,1,0:T(8,128)S(1)} all-to-all(f32[16,72,128]{2,1,0:T(8,128)S(1)} %route.1), channel_id=1, replica_groups=mesh['gx_0'=4,'gx_1'=8,'gy'=4,'gz'=2] {'gx_0','gy'}, dimensions={0} | all-to-all | bytes 1179648 | tf_op jit(solution)/shard_map/all_to_all | solution.py:531
  51.9 0.0 copy-done
  51.9 0.0 copy-done.2
  51.9 0.0 copy-done.3
  51.9 0.0 copy-done.4
  52.0 0.0 copy-done.5
  52.0 0.0 copy-done.6
  52.0 2.2 %update.1 = (f32[192,256]{1,0:T(8,128)}, f32[8,48,128]{2,1,0:T(8,128)S(1)}) custom-call(s32[8,128]{1,0:T(8,128)S(1)} %get-tuple-element.8.table, f32[16,72,128]{2,1,0:T(8,128)S(1)} %all_to_all.21.rcv, f32[192,256]{1,0:T(8,128)S(1)} %bitcast.17, f32[64,256]{1,0:T(8,128)S(1)} %bitcast.18, f32[64,40]{1,0:T(8,128)S(1)} %copy-done.6, f32[128,768]{1,0:T(8,128)S(1)} %copy-done.2, ...), custom_call_target="tpu_custom_call" | custom-call | tf_op jit(solution)/shard_map/update/pallas_call | solution.py:532
  54.1 12.2 %all_to_all.22.held = f32[8,48,128]{2,1,0:T(8,128)S(1)} all-to-all(f32[8,48,128]{2,1,0:T(8,128)S(1)} %get-tuple-element.13), channel_id=1, replica_groups=mesh['gx_0'=4,'gx_1'=8,'gy'=4,'gz'=2] {'gx_1'}, dimensions={0} | all-to-all | bytes 393216 | tf_op jit(solution)/shard_map/all_to_all | solution.py:545
  66.3 1.0 %send_back.1 = f32[16,48,128]{2,1,0:T(8,128)S(1)} custom-call(s32[8,128]{1,0:T(8,128)S(1)} %get-tuple-element.8.table, f32[8,48,128]{2,1,0:T(8,128)S(1)} %all_to_all.22.held), custom_call_target="tpu_custom_call" | custom-call | tf_op jit(solution)/shard_map/send_back/pallas_call | solution.py:546
  67.3 11.9 %all_to_all.23.rcv = f32[16,48,128]{2,1,0:T(8,128)S(1)} all-to-all(f32[16,48,128]{2,1,0:T(8,128)S(1)} %send_back.1), channel_id=1, replica_groups=mesh['gx_0'=4,'gx_1'=8,'gy'=4,'gz'=2] {'gx_0','gy'}, dimensions={0} | all-to-all | bytes 786432 | tf_op jit(solution)/shard_map/all_to_all | solution.py:553
  79.1 2.5 %place.1 = f32[96,32,256]{2,1,0:T(8,128)} custom-call(s32[8,128]{1,0:T(8,128)S(1)} %get-tuple-element.8.table, f32[16,48,128]{2,1,0:T(8,128)S(1)} %all_to_all.23.rcv, f32[96,32,256]{2,1,0:T(8,128)} %bitcast.14), custom_call_target="tpu_custom_call", output_to_operand_aliasing={{}: (2, {})} | custom-call | tf_op jit(solution)/shard_map/place/pallas_call | solution.py:554
  (3 shorter events, 0.0 us)
Async XLA Ops:
  0.6 2.0 %copy-start.7 = (f32[40,128]{1,0:T(8,128)S(1)}, f32[40,128]{1,0:T(8,128)}, u32[]{:S(2)}) copy-start(f32[40,128]{1,0:T(8,128)} %constant.10.clone.const) | copy-start | bytes 61444
  0.6 2.0 %copy-start.1 = (f32[3,4,16,256]{3,2,1,0:T(8,128)S(1)}, f32[3,4,16,256]{3,2,1,0:T(8,128)}, u32[]{:S(2)}) copy-start(f32[3,4,16,256]{3,2,1,0:T(8,128)} %param.12) | copy-start | bytes 589828
  0.7 2.0 %copy-start.8 = (s32[512,3]{0,1:T(4,128)S(1)}, s32[512,3]{0,1:T(4,128)}, u32[]{:S(2)}) copy-start(s32[512,3]{0,1:T(4,128)} %param.14) | copy-start | bytes 18436
  0.7 2.0 %copy-start.10 = (s32[512]{0:T(512)S(1)}, s32[512]{0:T(512)}, u32[]{:S(2)}) copy-start(s32[512]{0:T(512)} %param.15) | copy-start | bytes 6148
  0.7 2.0 %copy-start.9 = (s32[512,2]{0,1:T(2,128)S(1)}, s32[512,2]{0,1:T(2,128)}, u32[]{:S(2)}) copy-start(s32[512,2]{0,1:T(2,128)} %param.16) | copy-start | bytes 12292
  2.6 49.3 %copy-start = (f32[3,32,32,256]{3,2,1,0:T(8,128)}, f32[3,32,32,256]{3,2,1,0:T(8,128)S(1)}, u32[]{:S(2)}) copy-start(f32[3,32,32,256]{3,2,1,0:T(8,128)S(1)} %copy.16) | copy-start | bytes 9437188
  2.7 49.3 %copy-start.2 = (f32[128,768]{1,0:T(8,128)S(1)}, f32[128,768]{1,0:T(8,128)}, u32[]{:S(2)}) copy-start(f32[128,768]{1,0:T(8,128)} %constant.12.clone.faces) | copy-start | bytes 1179652
  2.7 49.3 %copy-start.3 = (f32[2,256,128]{2,1,0:T(8,128)S(1)}, f32[2,256,128]{2,1,0:T(8,128)}, u32[]{:S(2)}) copy-start(f32[2,256,128]{2,1,0:T(8,128)} %constant.14.clone.pool) | copy-start | bytes 786436
  2.7 49.3 %copy-start.4 = (f32[128,256]{1,0:T(8,128)S(1)}, f32[128,256]{1,0:T(8,128)}, u32[]{:S(2)}) copy-start(f32[128,256]{1,0:T(8,128)} %constant.13.clone.ends) | copy-start | bytes 393220
  2.7 49.2 %copy-start.5 = (f32[4,16,256]{2,1,0:T(8,128)S(1)}, f32[4,16,256]{2,1,0:T(8,128)}, u32[]{:S(2)}) copy-start(f32[4,16,256]{2,1,0:T(8,128)} %param.13) | copy-start | bytes 196612
  2.7 49.2 %copy-start.6 = (f32[64,40]{1,0:T(8,128)S(1)}, f32[64,40]{1,0:T(8,128)}, u32[]{:S(2)}) copy-start(f32[64,40]{1,0:T(8,128)} %constant.11.clone.along_x) | copy-start | bytes 30724
  5.5 1.4 %collective-permute-start = (f32[144,128]{1,0:T(8,128)S(1)}, f32[144,128]{1,0:T(8,128)S(1)}, u32[]{:S(2)}, u32[]{:S(2)}) collective-permute-start(f32[144,128]{1,0:T(8,128)S(1)} %get-tuple-element.10), channel_id=1, source_target_pairs={{0,1},{1,0},{2,3},{3,2},{4,5},{5,4},{6,7},{7,6},{8,9},{9,8},{10,11... | collective-permute-start | bytes 221192 | tf_op jit(solution)/shard_map/ppermute | solution.py:511
  6.9 5.9 %collective-permute-start.2 = (f32[48,128]{1,0:T(8,128)S(1)}, f32[48,128]{1,0:T(8,128)S(1)}, u32[]{:S(2)}, u32[]{:S(2)}) collective-permute-start(f32[48,128]{1,0:T(8,128)S(1)} %get-tuple-element.14), channel_id=1, source_target_pairs={{2,0},{4,2},{6,4},{3,1},{5,3},{7,5},{10,8},{12,10},{14,12},{11,9},... | collective-permute-start | bytes 73736 | tf_op jit(solution)/shard_map/ppermute | solution.py:514
  8.2 6.1 %collective-permute-start.1 = (f32[48,128]{1,0:T(8,128)S(1)}, f32[48,128]{1,0:T(8,128)S(1)}, u32[]{:S(2)}, u32[]{:S(2)}) collective-permute-start(f32[48,128]{1,0:T(8,128)S(1)} %get-tuple-element.15), channel_id=1, source_target_pairs={{0,2},{2,4},{4,6},{1,3},{3,5},{5,7},{8,10},{10,12},{12,14},{9,11},... | collective-permute-start | bytes 73736 | tf_op jit(solution)/shard_map/ppermute | solution.py:513
where the time goes:
time: 82 us; the launch traced here: 81.7 us
  blocking collectives  60.9 us (74%)
  Pallas kernels  9.27 us (11%)
  starting transfers between devices  5.93 us (7%)
  waiting for transfers between devices  2.75 us (3%)
  local copies, waits for them, and re-layouts  2.03 us (2%)
  between operations  0.83 us (1%)
    all_to_all x1, blocking collectives, on_device(): held = lax.all_to_all(payload, 'gx_1', 0, 0)  20.8 us
    all_to_all x1, blocking collectives, on_device(): received = lax.all_to_all(routed, ('gx_0', 'gy'), 0, 0)  16.1 us
    all_to_all x1, blocking collectives, on_device(): held_means = lax.all_to_all(means, 'gx_1', 0, 0)  12.2 us
    all_to_all x1, blocking collectives, on_device(): returned = lax.all_to_all(back, ('gx_0', 'gy'), 0, 0)  11.9 us
    ppermute x1, starting transfers between devices, on_device(): above = lax.ppermute(halo[2], 'gy', [(i, i + 1) for i in range(LINE_Y - 1)])  4.55 us
    pallas_call x1, Pallas kernels, on_device(): pl.pallas_call(pack_kernel, out_shape=(shape(8, 128, dtype=i32), shape(3...  2.75 us
    pallas_call x1, Pallas kernels, on_device(): pl.pallas_call(place_kernel, out_shape=shape(96, 32, 256), in_specs=[smem...  2.52 us
    pallas_call x1, Pallas kernels, on_device(): pl.pallas_call(update_kernel, out_shape=(shape(3 * SLOTS * F, F * F), sha...  2.17 us
  transfers between devices with their start and end apart: 3, of which 2 were waited for; matrix products, arithmetic and copies ran while one was open for 0% of the time, Pallas kernels for 0%

commit v1 on v0

--- a/solution.py
+++ b/solution.py
@@ -17,8 +17,9 @@
 LINE_Z = 8
 LINE_Y = 4
 PLANE = LINE_X * LINE_Y
-HALO = 48
+PACKED = 80
 SEND = 72
+FIRST = SEND + 16
 HIGHEST = lax.Precision.HIGHEST
 step_rate = 0.15
 f32 = jnp.float32
@@ -80,12 +81,21 @@
         out[24 + k, [60 + 10 * k, 90 + 10 * k]] = 1.0
         out[27 + k, 30 + 10 * k : 40 + 10 * k] = 0.75
         out[27 + k, [69 + 10 * k, 99 + 10 * k]] = 1.0
+    beside = np.zeros((128, 128))
+    for face in range(2):
+        for k in range(3):
+            for c in range(SIDE):
+                at = face * 30 + k * 10 + c
+                edge = face * 9 + 10 * k
+                beside[at, at] = 0.75
+                beside[at, 60 + edge] = {0: 0.75, 1: 0.25}.get(c, 0.0)
+                beside[at, 90 + edge] = {9: 0.75, 8: 0.25}.get(c, 0.0)
     lanes = np.arange(128)
     out[32] = np.where(lanes < 60, lanes % 10, np.where(lanes < 90, 0, np.where(lanes < 120, 9, -999)))
     out[33] = np.where(lanes < 60, -999, np.where(lanes < 90, 1, np.where(lanes < 120, 8, -999)))
     out[34] = np.where(lanes < 60, 1.0, 0.75)
     out[35] = 0.25
-    return out.astype(np.float32)
+    return out.astype(np.float32), beside.astype(np.float32)
 
 
 def position():
@@ -103,8 +113,8 @@
     home = gx * LINE_Y + gy
     brick_key = (home * 2 + gz) * SLOTS + box
     word = (1 + box * 2 + home * 8 + (low + 1) * 1024).astype(f32)
-    sub = lax.broadcasted_iota(i32, (64, 1), 0)
-    eye = (lax.broadcasted_iota(i32, (64, 128), 0) == lax.broadcasted_iota(i32, (64, 128), 1)).astype(f32)
+    sub = lax.broadcasted_iota(i32, (32, 1), 0)
+    eye = (lax.broadcasted_iota(i32, (32, 128), 0) == lax.broadcasted_iota(i32, (32, 128), 1)).astype(f32)
 
     def to_row(column):
         return jnp.sum(eye * column, axis=0, keepdims=True)
@@ -113,7 +123,7 @@
         return jnp.sum(jnp.where(match, values, 0.0), axis=1, keepdims=True)
 
     def device_of(j):
-        return (((j >> 2) * LINE_Z + my_z) * LINE_Y + (j & 3)) * 2 + my_c
+        return ((my_x * LINE_Z + j) * LINE_Y + my_y) * 2 + my_c
 
     keys = device_of(sub >> 2) * SLOTS + (sub & 3)
     held = keys == gs
@@ -133,7 +143,7 @@
     mine = device_of(sub >> 2)
     my_mask = boxes_on(mine)
     my_box = (words.astype(i32) >> 1) & 3
-    lanes = lax.broadcasted_iota(i32, (64, 128), 1)
+    lanes = lax.broadcasted_iota(i32, (32, 128), 1)
     same_j = (sub >> 2) == (lanes >> 2)
     route_row = jnp.zeros((1, 128), f32)
     sends_row = jnp.zeros((1, 128), f32)
@@ -155,17 +165,19 @@
         else:
             here, there = 2 + after(my_mask, my_box), before(near_mask, near_box)
         target = jnp.where(same_j & ((lanes & 3) == here) & outer, 1.0, 0.0)
-        code = (((device >> 3) & 7) * 4 + there + 1).astype(f32)
+        plane = (device >> 6) * LINE_Y + ((device >> 1) & 3)
+        code = (plane * 4 + there + 1).astype(f32)
         route_row = route_row + jnp.sum(target * code, axis=0, keepdims=True)
         sends_row = sends_row + jnp.sum(target * ((sub & 3) + 1).astype(f32), axis=0, keepdims=True)
-        plane = (device >> 6) * LINE_Y + ((device >> 1) & 3)
-        word = jnp.where(outer, 2 + here * 4 + plane * 16, 1 + ((slot - 1) & 3) * 4)
+        word = jnp.where(outer, 2 + here * 4 + ((device >> 3) & 7) * 16, 1 + ((slot - 1) & 3) * 4)
         near_words.append(jnp.where(slot > 0, word, 0).astype(f32))
     owner = pick(keys == brick_key, slot_plus)
-    sub16 = lax.broadcasted_iota(i32, (16, 1), 0)
-    on_device = device_of(sub16) == (gs >> 2)
-    homes = jnp.max(jnp.where(on_device, (home + 1).astype(f32), 0.0), axis=1, keepdims=True)
-    homes = jnp.concatenate([homes, jnp.zeros((48, 1), f32)], axis=0)
+    sub8 = lax.broadcasted_iota(i32, (8, 1), 0)
+    on_device = device_of(sub8) == (gs >> 2)
+    in_y = cy & 31
+    side_y = jnp.where(in_y == 0, 128, jnp.where(in_y == 24, 256, 0))
+    homes = jnp.max(jnp.where(on_device, (home + 1 + side_y).astype(f32), 0.0), axis=1, keepdims=True)
+    homes = jnp.concatenate([homes, jnp.zeros((24, 1), f32)], axis=0)
     sub24 = lax.broadcasted_iota(i32, (24, 1), 0)
     target_x = my_x * LINE_Z + my_z + jnp.where(sub24 >= 12, 1, jnp.where(sub24 >= 6, 0, -1))
     target_x = jnp.where(sub24 >= 18, -1, target_x)
@@ -175,7 +187,7 @@
     near_brick = (target_x == gx) & (target_y == gy) & (target_z == gz)
     place = ((cy & 31) * 256 + (cz & 255)).astype(f32)
     anchors = jnp.max(jnp.where(near_brick, place, -1.0), axis=1, keepdims=True)
-    anchors = jnp.concatenate([anchors, jnp.zeros((40, 1), f32)], axis=0)
+    anchors = jnp.concatenate([anchors, jnp.zeros((8, 1), f32)], axis=0)
     rows = [to_row(v) for v in (words, homes, *near_words, owner, anchors)] + [route_row, sends_row]
     for r, row in enumerate(rows):
         table_ref[r : r + 1, :] = row.astype(i32)
@@ -183,7 +195,7 @@
 
 def pack_kernel(
     corners_ref, slots_ref, near_ref, fine_ref, brick, const,
-    table_ref, own_ref, other_ref, planes_ref,
+    table_ref, own_ref, other_ref, planes_ref, window_ref,
     table, table_sem,
 ):
     make_table(corners_ref, slots_ref, near_ref, table_ref)
@@ -193,7 +205,7 @@
     other_ref[...] = jnp.zeros_like(other_ref)
     planes_ref[...] = jnp.zeros_like(planes_ref)
     fetch.wait()
-    me = lax.axis_index("gx_0") * LINE_Y + lax.axis_index("gy")
+    me = lax.axis_index("gx_1")
     for e in range(4):
         s = jnp.maximum(table[ROW_SENDS, me * 4 + e] - 1, 0)
         for k in range(3):
@@ -219,16 +231,11 @@
     def tile_row(y):
         return (y >> 3) * 16 + (y & 7)
 
-    def layers(dy, y0):
-        if dy == 0:
-            for t in range(SIDE):
-                y = y0 - 1 + t
-                valid = True if 0 < t < SIDE - 1 else (y >= 0) & (y < 32)
-                yield t, jnp.clip(y, 0, 31), valid
-        elif dy == 1:
-            yield 0, 31, y0 == 0
-        else:
-            yield SIDE - 1, 0, y0 == 24
+    def layers(y0):
+        for t in range(SIDE):
+            y = y0 - 1 + t
+            valid = True if 0 < t < SIDE - 1 else (y >= 0) & (y < 32)
+            yield t, jnp.clip(y, 0, 31), valid
 
     weights = {0: (0.75, 0), 1: (0.25, 0), SIDE - 2: (0.25, 30), SIDE - 1: (0.75, 30)}
 
@@ -237,18 +244,21 @@
         high = 0.75 * u[:, 9:10] + 0.25 * u[:, 8:9]
         return low, high
 
-    def main_rows(dy, y0, z_base):
+    def beside_rows(dy, z_base):
         total = jnp.zeros((32, 128), f32)
-        for t, y, valid in layers(dy, y0):
-            for k in range(3):
-                u = shifted(k * 2048 + tile_row(y), 32, 64, z_base, valid)
-                low, high = ends_of(u)
-                total = jnp.where(lane == 60 + 10 * k + t, low, total)
-                total = jnp.where(lane == 90 + 10 * k + t, high, total)
-                if t in weights:
-                    w, face = weights[t]
-                    total = total + w * (pltpu.roll(u, face + 10 * k, 1) if face + k else u)
+        y, face = (31, 0) if dy == 1 else (0, 30)
+        for k in range(3):
+            u = shifted(k * 2048 + tile_row(y), 32, 64, z_base, True)
+            total = total + (pltpu.roll(u, face + 10 * k, 1) if face + k else u)
         return total
+
+    def diagonal_row(x, dy, z_base):
+        y, face = (31, 0) if dy == 1 else (0, 30)
+        face += 0 if x else 60
+        u = shifted(x * 64 + tile_row(y), 3, 2048, z_base, True)
+        row = jnp.where(sub3 == 0, u, jnp.where(sub3 == 1, pltpu.roll(u, 10, 1), pltpu.roll(u, 20, 1)))
+        row = jnp.sum(row, axis=0, keepdims=True)
+        return pltpu.roll(row, face, 1) if face else row
 
     def all_rows(y0, z_base):
         offset = lax.broadcasted_iota(i32, (256, 1), 0) - z_base
@@ -277,10 +287,10 @@
             rows = rows + low * cells[768 + 32 * k : 800 + 32 * k] + high * cells[864 + 32 * k : 896 + 32 * k]
         return rows
 
-    def edge_rows(x, dy, y0, z_base, with_row):
+    def edge_rows(x, y0, z_base, with_row):
         flat = jnp.zeros((3, 128), f32)
         row = jnp.zeros((3, 128), f32)
-        for t, y, valid in layers(dy, y0):
+        for t, y, valid in layers(y0):
             u = shifted(x * 64 + tile_row(y), 3, 2048, z_base, valid)
             flat = flat + (pltpu.roll(u, 10 * t, 1) if t else u)
             if with_row:
@@ -301,7 +311,6 @@
         out = other_ref if dz else own_ref
         z_shift = 256 * (1 - 2 * my_c) if dz else 0
         for dy in (-1, 0, 1):
-            base = (dy + 1) * HALO
             for dx in (0, -1, 1):
                 place = table[ROW_ANCHOR, (dx + 1) * 6 + (dy + 1) * 2 + dz]
                 y0, z0 = place >> 8, place & 255
@@ -315,17 +324,26 @@
                     near &= z0 == jnp.where(my_c == 0, 0, 248)
 
                 @pl.when(near)
-                def _(out=out, base=base, dx=dx, dy=dy, y0=y0, z_base=z_base):
-                    if dx == 0:
-                        out[base : base + 32, :] = main_rows(dy, y0, z_base) if dy else all_rows(y0, z_base)
-                        for x, at in ((0, 0), (31, 3)):
-                            flat, _row = edge_rows(x, dy, y0, z_base, False)
-                            out[base + 32 + at : base + 35 + at, :] = 0.25 * flat
-                    else:
-                        x, at = (0, base + 44) if dx == -1 else (31, base + 40)
-                        flat, row = edge_rows(x, dy, y0, z_base, True)
+                def _(out=out, dz=dz, dx=dx, dy=dy, y0=y0, z0=z0, z_base=z_base):
+                    if dy and dx:
+                        out[38:39, :] += diagonal_row(0 if dx == -1 else 31, dy, z_base)
+                    elif dy:
+                        out[48:80, :] += beside_rows(dy, z_base)
+                    elif dx:
+                        x, at = (0, 44) if dx == -1 else (31, 40)
+                        flat, row = edge_rows(x, y0, z_base, True)
                         out[at : at + 3, :] = 0.75 * flat
                         out[at + 3 : at + 4, :] = row
+                    else:
+                        out[0:32, :] = all_rows(y0, z_base)
+                        for x, at in ((0, 32), (31, 35)):
+                            flat, _row = edge_rows(x, y0, z_base, False)
+                            out[at : at + 3, :] = 0.25 * flat
+                        if dz == 0:
+                            start = (y0 >> 3) * 16 + (z0 >> 7) * 8
+                            for n in range(96):
+                                tile = brick[pl.ds(pl.multiple_of(n * 64 + start, 8), 8), :]
+                                window_ref[n * 8 : n * 8 + 8, :] = tile
 
 
 def split_slot(slot):
@@ -333,30 +351,72 @@
     return device >> 6, (device >> 3) & 7, (device >> 1) & 3, slot & 3
 
 
-def join_kernel(middle, above, below, planes, out):
-    total = middle[...] + above[...] + below[...]
+def join_kernel(own, other, planes, out):
+    total = own[...] + other[...]
     sub = lax.broadcasted_iota(i32, (8, 1), 0)
     tiles = []
     for e in range(4):
         pair = jnp.where(sub == 6, total[40 + 2 * e : 41 + 2 * e], total[41 + 2 * e : 42 + 2 * e])
         tiles.append(jnp.where(sub < 6, planes[e * 8 : e * 8 + 8, :], pair))
-    payload = jnp.concatenate([total[:40]] + tiles, axis=0)
-    for z in range(LINE_Z):
-        out[z] = payload
-
-
-def route_kernel(table, held, out):
+    two = total[48:64] + pltpu.roll(total[64:80], 64, 1)
+    payload = jnp.concatenate([total[:40]] + tiles + [two], axis=0)
+    for j in range(PLANE):
+        out[j] = payload
+
+
+def route_kernel(table, held, beside_ref, out, rows, spread):
     sub = lax.broadcasted_iota(i32, (8, 1), 0)
-    for j in range(PLANE):
-        home = jnp.maximum(table[ROW_HOME, j] - 1, 0)
-        z = (home >> 2) & 7
-        out[j, 0:40] = held[z, 0:40]
-        for e in range(4):
-            code = jnp.maximum(table[ROW_ROUTE, j * 4 + e] - 1, 0)
-            start = pl.multiple_of(40 + (code & 3) * 8, 8)
-            at = 40 + e * 8
-            piece = held[(z + (7 if e < 2 else 1)) & 7, at : at + 8]
-            out[j, at : at + 8] = jnp.where(sub < 6, held[code >> 2, pl.ds(start, 8)], piece)
+    lane = lax.broadcasted_iota(i32, (1, 128), 1)
+
+    def line_of(gx):
+        return (jnp.clip(gx, 0, 31) >> 3) * LINE_Y
+
+    def read(j):
+        code = jnp.maximum(table[ROW_HOME, j] - 1, 0)
+        home, edge = code & 127, code >> 7
+        gx, gy = home >> 2, home & 3
+        near_y = jnp.where(edge == 1, gy - 1, gy + 1)
+        used = (edge > 0) & (near_y >= 0) & (near_y < LINE_Y)
+        start = jnp.where(edge == 2, 30, 0)
+        keep = (lane >= start) & (lane < start + 30) & used
+        return gx, gy, jnp.clip(near_y, 0, LINE_Y - 1), edge, keep
+
+    for j in range(LINE_Z):
+        gx, _, near_y, _, keep = read(j)
+        both = held[line_of(gx) + near_y, SEND:FIRST]
+        rows[j * 32 : j * 32 + 16, :] = jnp.where(keep, both, 0.0)
+        rows[j * 32 + 16 : j * 32 + 32, :] = jnp.where(keep, pltpu.roll(both, 64, 1), 0.0)
+        for side in range(2):
+            row = held[line_of(gx + (1 if side else -1)) + near_y, 32:40][6:7]
+            at = LINE_Z * 32 + j * 2 + side
+            rows[at : at + 1, :] = jnp.where(keep, pltpu.roll(row, 68, 1) if side else row, 0.0)
+    spread[...] = jnp.dot(rows[...], beside_ref[...], precision=HIGHEST, preferred_element_type=f32)
+
+    for j in range(LINE_Z):
+        gx, gy, _, edge, _ = read(j)
+        home_at = line_of(gx) + gy
+        shift = jnp.where(edge == 2, 60, 0)
+        kept = (lane >= jnp.where(edge == 2, 90, 0)) & (lane < jnp.where(edge == 2, 100, SIDE))
+
+        def flats(row):
+            return [jnp.where(kept, pltpu.roll(row, (shift + 128 - 10 * k) & 127, 1), 0.0) for k in range(3)]
+
+        out[j, 0:32] = held[home_at, 0:32] + spread[j * 32 : j * 32 + 32, :]
+        ends = held[home_at, 32:40]
+        for i, row in enumerate(flats(rows[j * 32 : j * 32 + 1, :]) + flats(rows[j * 32 + 31 : j * 32 + 32, :])):
+            ends = ends + jnp.where(sub == i, 0.25 * row, 0.0)
+        out[j, 32:40] = ends
+        for side in range(2):
+            at = LINE_Z * 32 + j * 2 + side
+            added = [0.75 * row for row in flats(rows[at : at + 1, :])] + [spread[at : at + 1, :]]
+            source = line_of(gx + (1 if side else -1)) + gy
+            for half in range(2):
+                e = side * 2 + half
+                code = jnp.maximum(table[ROW_ROUTE, j * 4 + e] - 1, 0)
+                start = pl.multiple_of(40 + (code & 3) * 8, 8)
+                tile = held[source, 40 + e * 8 : 48 + e * 8]
+                tile = tile + jnp.where(sub == 6, added[2 * half], jnp.where(sub == 7, added[2 * half + 1], 0.0))
+                out[j, 40 + e * 8 : 48 + e * 8] = jnp.where(sub < 6, held[code >> 2, pl.ds(start, 8)], tile)
 
 
 def update_kernel(
@@ -364,13 +424,9 @@
     fine_out, means_out,
     sums, planes, advanced, pooled,
 ):
-    my_x, _, my_y, _ = position()
-    me = my_x * LINE_Y + my_y
-    home = jnp.maximum(table[ROW_HOME, me] - 1, 0)
-    gx, hy = home >> 2, home & 3
-    at_home = (gx >> 3) * LINE_Y + hy
-    at_low = (jnp.maximum(gx - 1, 0) >> 3) * LINE_Y + hy
-    at_high = (jnp.minimum(gx + 1, 31) >> 3) * LINE_Y + hy
+    me = lax.axis_index("gx_1")
+    gx = (jnp.maximum(table[ROW_HOME, me] - 1, 0) & 127) >> 2
+    at_home, at_low, at_high = gx & 7, (gx + 7) & 7, (gx + 1) & 7
     sub8 = lax.broadcasted_iota(i32, (8, 1), 0)
 
     def piece_rows(at, tile, inside):
@@ -427,26 +483,25 @@
             advanced[at + 48 : at + 96, :], pool[1]
         )
     means = pooled[pl.ds(0, 48, stride=2), :] + pooled[pl.ds(1, 48, stride=2), :]
-    for z in range(LINE_Z):
-        means_out[z] = means
+    for j in range(PLANE):
+        means_out[j] = means
 
 
 def return_kernel(table, held, out):
     first = lax.broadcasted_iota(i32, (1, 128), 1) < 64
-    for j in range(PLANE):
+    for j in range(LINE_Z):
         for p in range(2):
             picks = []
             for h in range(2):
-                _, z, _, local = split_slot(jnp.maximum(table[ROW_OWNER, j * 4 + 2 * p + h] - 1, 0))
+                x, _, y, local = split_slot(jnp.maximum(table[ROW_OWNER, j * 4 + 2 * p + h] - 1, 0))
                 start = pl.multiple_of((local >> 1) * 24, 8)
-                rows = held[z, pl.ds(start, 24)]
+                rows = held[x * LINE_Y + y, pl.ds(start, 24)]
                 picks.append(jnp.where((local & 1) == h, rows, pltpu.roll(rows, 64, 1)))
             out[j, p * 24 : p * 24 + 24] = jnp.where(first, picks[0], picks[1])
 
 
-def place_kernel(table, rcv, coarse_ref, coarse_out, window, spread, sem):
-    my_x, _, my_y, _ = position()
-    me = my_x * LINE_Y + my_y
+def place_kernel(table, rcv, window, coarse_ref, coarse_out, spread, sem):
+    me = lax.axis_index("gx_1")
     place = table[ROW_ANCHOR, SELF_TARGET]
 
     @pl.when(place >= 0)
@@ -456,22 +511,17 @@
         z_tile = pl.multiple_of((z0 >> 7) * 128, 128)
         z_in = z0 & 127
         region = coarse_out.at[:, pl.ds(y0, 8), pl.ds(z_tile, 128)]
-        load = pltpu.make_async_copy(region, window, sem.at[0])
-        load.start()
         for i in range(SLOTS):
-            ox, _, oy, _ = split_slot(jnp.maximum(table[ROW_OWNER, me * 4 + i] - 1, 0))
-            at = ox * LINE_Y + oy
+            _, at, _, _ = split_slot(jnp.maximum(table[ROW_OWNER, me * 4 + i] - 1, 0))
             for k in range(3):
                 start = ((i // 2) * 3 + k) * 8
                 values = rcv[at, start : start + 8]
                 for b in range(B):
                     shift = (z_in + 256 - (b * B + 64 * (i % 2))) & 127
                     spread[pl.ds((k * 32 + i * B) * B + b, B, stride=B), :] = pltpu.roll(values, shift, 1)
-        load.wait()
-        lane = lax.broadcasted_iota(i32, (1, 1, 128), 2)
-        fresh = spread[...].reshape(96, 8, 128)
-        window[...] = jnp.where((lane >= z_in) & (lane < z_in + B), fresh, window[...])
-        store = pltpu.make_async_copy(window, region, sem.at[1])
+        lane = lax.broadcasted_iota(i32, (1, 128), 1)
+        spread[...] = jnp.where((lane >= z_in) & (lane < z_in + B), spread[...], window[...])
+        store = pltpu.make_async_copy(spread.reshape(96, 8, 128), region, sem)
         store.start()
         store.wait()
 
@@ -495,43 +545,44 @@
 def on_device(coarse_field, fine_field, viscosity, corners, grid_slot, neighbors):
     fine = fine_field.reshape(3 * SLOTS * F, F * F)
     tiles = coarse_field.reshape(3, 32, 4, 8, 2, 128).transpose(0, 1, 2, 4, 3, 5).reshape(6144, 128)
-    table, own, other, planes = pl.pallas_call(
+    pack_const, beside = map(jnp.asarray, pack_constants())
+    table, own, other, planes, window = pl.pallas_call(
         pack_kernel,
         out_shape=(
             shape(8, 128, dtype=i32),
-            shape(3 * HALO, 128),
-            shape(3 * HALO, 128),
+            shape(PACKED, 128),
+            shape(PACKED, 128),
             shape(32, 128),
+            shape(768, 128),
         ),
         in_specs=[vmem()] * 6,
-        out_specs=(vmem(), vmem(), vmem(), vmem()),
+        out_specs=(vmem(),) * 5,
         scratch_shapes=[pltpu.SMEM((8, 128), i32), pltpu.SemaphoreType.DMA(())],
         name="pack", compiler_params=pltpu.CompilerParams(vmem_limit_bytes=24 << 20),
-    )(corners.T, grid_slot[None, :], neighbors.T, fine, tiles, jnp.asarray(pack_constants()))
-    halo = own + lax.ppermute(other, "gz", [(0, 1), (1, 0)])
-    halo = halo.reshape(3, HALO, 128)
-    above = lax.ppermute(halo[2], "gy", [(i, i + 1) for i in range(LINE_Y - 1)])
-    below = lax.ppermute(halo[0], "gy", [(i + 1, i) for i in range(LINE_Y - 1)])
+    )(corners.T, grid_slot[None, :], neighbors.T, fine, tiles, pack_const)
+    other = lax.ppermute(other, "gz", [(0, 1), (1, 0)])
     payload = pl.pallas_call(
         join_kernel,
-        out_shape=shape(LINE_Z, SEND, 128),
-        in_specs=[vmem()] * 4,
+        out_shape=shape(PLANE, FIRST, 128),
+        in_specs=[vmem()] * 3,
         out_specs=vmem(),
         name="join",
         compiler_params=pltpu.CompilerParams(vmem_limit_bytes=8 << 20),
-    )(halo[1], above, below, planes)
-    held = lax.all_to_all(payload, "gx_1", 0, 0)
+    )(own, other, planes)
+    held = lax.all_to_all(payload, ("gx_0", "gy"), 0, 0)
     routed = pl.pallas_call(
         route_kernel,
-        out_shape=shape(PLANE, SEND, 128),
-        in_specs=[smem(), vmem()],
+        out_shape=shape(LINE_Z, SEND, 128),
+        in_specs=[smem(), vmem(), vmem()],
         out_specs=vmem(),
-        name="route", compiler_params=pltpu.CompilerParams(vmem_limit_bytes=8 << 20),
-    )(table, held)
-    received = lax.all_to_all(routed, ("gx_0", "gy"), 0, 0)
+        scratch_shapes=[pltpu.VMEM((LINE_Z * 34, 128), f32)] * 2,
+        name="route",
+        compiler_params=pltpu.CompilerParams(vmem_limit_bytes=8 << 20),
+    )(table, held, beside)
+    received = lax.all_to_all(routed, "gx_1", 0, 0)
     fine_out, means = pl.pallas_call(
         update_kernel,
-        out_shape=(shape(3 * SLOTS * F, F * F), shape(LINE_Z, 48, 128)),
+        out_shape=(shape(3 * SLOTS * F, F * F), shape(PLANE, 48, 128)),
         in_specs=[smem()] + [vmem()] * 7,
         out_specs=(vmem(), vmem()),
         scratch_shapes=[
@@ -542,28 +593,24 @@
         ],
         name="update", compiler_params=pltpu.CompilerParams(vmem_limit_bytes=16 << 20),
     )(table, received, fine, viscosity.reshape(SLOTS * F, F * F), *map(jnp.asarray, constant_matrices()))
-    held_means = lax.all_to_all(means, "gx_1", 0, 0)
+    held_means = lax.all_to_all(means, ("gx_0", "gy"), 0, 0)
     back = pl.pallas_call(
         return_kernel,
-        out_shape=shape(PLANE, 48, 128),
+        out_shape=shape(LINE_Z, 48, 128),
         in_specs=[smem(), vmem()],
         out_specs=vmem(),
         name="send_back", compiler_params=pltpu.CompilerParams(vmem_limit_bytes=8 << 20),
     )(table, held_means)
-    returned = lax.all_to_all(back, ("gx_0", "gy"), 0, 0)
+    returned = lax.all_to_all(back, "gx_1", 0, 0)
     coarse_out = pl.pallas_call(
         place_kernel,
         out_shape=shape(96, 32, 256),
-        in_specs=[smem(), vmem(), anywhere()],
+        in_specs=[smem(), vmem(), vmem(), anywhere()],
         out_specs=anywhere(),
-        input_output_aliases={2: 0},
-        scratch_shapes=[
-            pltpu.VMEM((96, 8, 128), f32),
-            pltpu.VMEM((768, 128), f32),
-            pltpu.SemaphoreType.DMA((2,)),
-        ],
+        input_output_aliases={3: 0},
+        scratch_shapes=[pltpu.VMEM((768, 128), f32), pltpu.SemaphoreType.DMA(())],
         name="place", compiler_params=pltpu.CompilerParams(vmem_limit_bytes=8 << 20),
-    )(table, returned, coarse_field.reshape(96, 32, 256))
+    )(table, returned, window, coarse_field.reshape(96, 32, 256))
     return fine_out.reshape(fine_field.shape), coarse_out.reshape(coarse_field.shape)
 
 

time: 82 us -> 77 us (0.939); the launches traced: 81.7 us -> 75.7 us
  starting transfers between devices: 5.93 us -> 1.19 us
  blocking collectives: 60.9 us -> 64.6 us
  Pallas kernels: 9.27 us -> 6.22 us
  waiting for transfers between devices: 2.75 us -> 0.87 us
    ppermute x3 -> x1, starting transfers between devices: 5.93 us -> 1.19 us  [on_device(): other = lax.ppermute(other, 'gz', [(0, 1), (1, 0)])]
    all_to_all x4, blocking collectives: 60.9 us -> 64.6 us  [the longest x1 19.8 us: on_device(): held = lax.all_to_all(payload, ('gx_0', 'gy'), 0, 0)]
    pallas_call x1, Pallas kernels: 2.52 us -> 0.62 us  [on_device(): pl.pallas_call(place_kernel, out_shape=shape(96, 32, 256), in_specs=[smem...]
    ppermute x3 -> x1, waiting for transfers between devices: 2.75 us -> 0.87 us  [on_device(): other = lax.ppermute(other, 'gz', [(0, 1), (1, 0)])]
    pallas_call x4, Pallas kernels: 4.58 us -> 3.42 us  [the longest x1 1.45 us: on_device(): pl.pallas_call(pack_kernel, out_shape=(shape(8, 128, dtype=i32), shape(PA...]
    unnamed x23 -> x25, local copies, waits for them, and re-layouts: 2.02 us -> 2.02 us
  transfers between devices with their start and end apart: 3 -> 1, of which waited for: 2 -> 1; matrix products, arithmetic and copies ran while one was open for 0% -> 0% of each run, Pallas kernels for 0% -> 0%
where the time goes in v1:
time: 77 us; the launch traced here: 75.7 us
  blocking collectives  64.6 us (84%)
  Pallas kernels  6.22 us (8%)
  local copies, waits for them, and re-layouts  2.02 us (3%)
  starting transfers between devices  1.19 us (2%)
  waiting for transfers between devices  0.87 us (1%)
  between operations  0.79 us (1%)
    all_to_all x1, blocking collectives, on_device(): held = lax.all_to_all(payload, ('gx_0', 'gy'), 0, 0)  19.8 us
    all_to_all x1, blocking collectives, on_device(): received = lax.all_to_all(routed, 'gx_1', 0, 0)  19.8 us
    all_to_all x1, blocking collectives, on_device(): held_means = lax.all_to_all(means, ('gx_0', 'gy'), 0, 0)  12.9 us
    all_to_all x1, blocking collectives, on_device(): returned = lax.all_to_all(back, 'gx_1', 0, 0)  12.2 us
    pallas_call x1, Pallas kernels, on_device(): pl.pallas_call(update_kernel, out_shape=(shape(3 * SLOTS * F, F * F), sha...  2.18 us
    unnamed x25, local copies, waits for them, and re-layouts  2.02 us
  transfers between devices with their start and end apart: 1, of which 1 were waited for; matrix products, arithmetic and copies ran while one was open for 0% of the time, Pallas kernels for 0%

profile of v1, /device:TPU:2, one launch (start us, length us, event | category | flops | bytes accessed | tf_op | source)
XLA Modules:
  0.0 75.7 jit_solution(8350268219290415191)
XLA Ops:
  0.6 0.0 copy-start.8
  0.6 0.0 copy-start.1
  0.7 0.0 copy-start.9
  0.7 0.0 copy-start.11
  0.7 0.0 copy-start.10
  0.7 2.0 %copy.17 = f32[3,32,32,256]{3,2,1,0:T(8,128)S(1)} copy(f32[3,32,32,256]{3,2,1,0:T(8,128)} %param.12) | data formatting | bytes 6291456
  2.6 0.0 copy-start
  2.6 0.0 copy-start.5
  2.6 0.0 copy-done.8
  2.6 0.0 copy-done.1
  2.7 0.0 copy-done.9
  2.7 0.0 copy-done.11
  2.7 0.0 copy-done.10
  2.7 0.0 copy-start.2
  2.7 0.0 copy-start.3
  2.7 0.0 copy-start.4
  2.7 0.0 copy-start.6
  2.7 0.0 copy-start.7
  2.7 1.5 %pack.1 = (s32[8,128]{1,0:T(8,128)S(1)}, f32[80,128]{1,0:T(8,128)S(1)}, f32[80,128]{1,0:T(8,128)S(1)}, f32[32,128]{1,0:T(8,128)S(1)}, f32[768,128]{1,0:T(8,128)S(1)}) custom-call(s32[3,512]{1,0:T(4,128)S(1)} %bitcast.19, s32[1,512]{1,0:T(1,128)S(1)} %bitcast.21, s32[2,512]{1,0:T(2,128)S(1)} %bitcast.20, f32[192,256]{1,0:T(8,128)S(1)} %bitcast.16, ...), custom_call_target="tpu_custom_call" | custom-call | tf_op jit(solution)/shard_map/pack/pallas_call | solution.py:549
  4.2 1.2 %collective-permute-start = (f32[80,128]{1,0:T(8,128)S(1)}, f32[80,128]{1,0:T(8,128)S(1)}, u32[]{:S(2)}, u32[]{:S(2)}) collective-permute-start(f32[80,128]{1,0:T(8,128)S(1)} %get-tuple-element.11), channel_id=1, source_target_pairs={{0,1},{1,0},{2,3},{3,2},{4,5},{5,4},{6,7},{7,6},{8,9},{9,8},{10,11... | collective-permute-start | bytes 122888 | tf_op jit(solution)/shard_map/ppermute | solution.py:563
  5.4 0.9 %collective-permute-done.other = f32[80,128]{1,0:T(8,128)S(1)} collective-permute-done((f32[80,128]{1,0:T(8,128)S(1)}, f32[80,128]{1,0:T(8,128)S(1)}, u32[]{:S(2)}, u32[]{:S(2)}) %collective-permute-start) | collective-permute-done | bytes 40992 | tf_op jit(solution)/shard_map/ppermute | solution.py:563
  6.3 0.1 join.1
  6.3 19.8 %all_to_all.20.held = f32[16,88,128]{2,1,0:T(8,128)S(1)} all-to-all(f32[16,88,128]{2,1,0:T(8,128)S(1)} %join.1), channel_id=1, replica_groups=mesh['gx_0'=4,'gx_1'=8,'gy'=4,'gz'=2] {'gx_0','gy'}, dimensions={0} | all-to-all | bytes 1441792 | tf_op jit(solution)/shard_map/all_to_all | solution.py:572
  26.1 0.0 copy-done.5
  26.1 1.1 %route.1 = f32[8,72,128]{2,1,0:T(8,128)S(1)} custom-call(s32[8,128]{1,0:T(8,128)S(1)} %get-tuple-element.9.table, f32[16,88,128]{2,1,0:T(8,128)S(1)} %all_to_all.20.held, f32[128,128]{1,0:T(8,128)S(1)} %copy-done.5), custom_call_target="tpu_custom_call" | custom-call | tf_op jit(solution)/shard_map/route/pallas_call | solution.py:573
  27.2 0.0 copy-done
  27.2 19.8 %all_to_all.21.rcv = f32[8,72,128]{2,1,0:T(8,128)S(1)} all-to-all(f32[8,72,128]{2,1,0:T(8,128)S(1)} %route.1), channel_id=1, replica_groups=mesh['gx_0'=4,'gx_1'=8,'gy'=4,'gz'=2] {'gx_1'}, dimensions={0} | all-to-all | bytes 589824 | tf_op jit(solution)/shard_map/all_to_all | solution.py:582
  47.0 0.0 copy-done.2
  47.0 0.0 copy-done.3
  47.0 0.0 copy-done.4
  47.0 0.0 copy-done.6
  47.0 0.0 copy-done.7
  47.0 2.2 %update.1 = (f32[192,256]{1,0:T(8,128)}, f32[16,48,128]{2,1,0:T(8,128)S(1)}) custom-call(s32[8,128]{1,0:T(8,128)S(1)} %get-tuple-element.9.table, f32[8,72,128]{2,1,0:T(8,128)S(1)} %all_to_all.21.rcv, f32[192,256]{1,0:T(8,128)S(1)} %bitcast.17, f32[64,256]{1,0:T(8,128)S(1)} %bitcast.18, f32[64,40]{1,0:T(8,128)S(1)} %copy-done.7, f32[128,768]{1,0:T(8,128)S(1)} %copy-done.2, ...), custom_call_target="tpu_custom_call" | custom-call | tf_op jit(solution)/shard_map/update/pallas_call | solution.py:583
  49.2 12.9 %all_to_all.22.held = f32[16,48,128]{2,1,0:T(8,128)S(1)} all-to-all(f32[16,48,128]{2,1,0:T(8,128)S(1)} %get-tuple-element.14), channel_id=1, replica_groups=mesh['gx_0'=4,'gx_1'=8,'gy'=4,'gz'=2] {'gx_0','gy'}, dimensions={0} | all-to-all | bytes 786432 | tf_op jit(solution)/shard_map/all_to_all | solution.py:596
  62.1 0.8 %send_back.1 = f32[8,48,128]{2,1,0:T(8,128)S(1)} custom-call(s32[8,128]{1,0:T(8,128)S(1)} %get-tuple-element.9.table, f32[16,48,128]{2,1,0:T(8,128)S(1)} %all_to_all.22.held), custom_call_target="tpu_custom_call" | custom-call | tf_op jit(solution)/shard_map/send_back/pallas_call | solution.py:597
  62.9 12.2 %all_to_all.23.rcv = f32[8,48,128]{2,1,0:T(8,128)S(1)} all-to-all(f32[8,48,128]{2,1,0:T(8,128)S(1)} %send_back.1), channel_id=1, replica_groups=mesh['gx_0'=4,'gx_1'=8,'gy'=4,'gz'=2] {'gx_1'}, dimensions={0} | all-to-all | bytes 393216 | tf_op jit(solution)/shard_map/all_to_all | solution.py:604
  75.1 0.6 place.1
Async XLA Ops:
  0.6 2.0 %copy-start.8 = (f32[40,128]{1,0:T(8,128)S(1)}, f32[40,128]{1,0:T(8,128)}, u32[]{:S(2)}) copy-start(f32[40,128]{1,0:T(8,128)} %constant.12.clone.const) | copy-start | bytes 61444
  0.6 2.0 %copy-start.1 = (f32[3,4,16,256]{3,2,1,0:T(8,128)S(1)}, f32[3,4,16,256]{3,2,1,0:T(8,128)}, u32[]{:S(2)}) copy-start(f32[3,4,16,256]{3,2,1,0:T(8,128)} %param.13) | copy-start | bytes 589828
  0.7 2.0 %copy-start.9 = (s32[512,3]{0,1:T(4,128)S(1)}, s32[512,3]{0,1:T(4,128)}, u32[]{:S(2)}) copy-start(s32[512,3]{0,1:T(4,128)} %param.15) | copy-start | bytes 18436
  0.7 2.0 %copy-start.11 = (s32[512]{0:T(512)S(1)}, s32[512]{0:T(512)}, u32[]{:S(2)}) copy-start(s32[512]{0:T(512)} %param.16) | copy-start | bytes 6148
  0.7 2.0 %copy-start.10 = (s32[512,2]{0,1:T(2,128)S(1)}, s32[512,2]{0,1:T(2,128)}, u32[]{:S(2)}) copy-start(s32[512,2]{0,1:T(2,128)} %param.17) | copy-start | bytes 12292
  2.6 24.6 %copy-start = (f32[3,32,32,256]{3,2,1,0:T(8,128)}, f32[3,32,32,256]{3,2,1,0:T(8,128)S(1)}, u32[]{:S(2)}) copy-start(f32[3,32,32,256]{3,2,1,0:T(8,128)S(1)} %copy.17) | copy-start | bytes 9437188
  2.6 23.5 %copy-start.5 = (f32[128,128]{1,0:T(8,128)S(1)}, f32[128,128]{1,0:T(8,128)}, u32[]{:S(2)}) copy-start(f32[128,128]{1,0:T(8,128)} %constant.13.clone.beside_ref) | copy-start | bytes 196612
  2.7 44.3 %copy-start.2 = (f32[128,768]{1,0:T(8,128)S(1)}, f32[128,768]{1,0:T(8,128)}, u32[]{:S(2)}) copy-start(f32[128,768]{1,0:T(8,128)} %constant.15.clone.faces) | copy-start | bytes 1179652
  2.7 44.3 %copy-start.3 = (f32[2,256,128]{2,1,0:T(8,128)S(1)}, f32[2,256,128]{2,1,0:T(8,128)}, u32[]{:S(2)}) copy-start(f32[2,256,128]{2,1,0:T(8,128)} %constant.17.clone.pool) | copy-start | bytes 786436
  2.7 44.3 %copy-start.4 = (f32[128,256]{1,0:T(8,128)S(1)}, f32[128,256]{1,0:T(8,128)}, u32[]{:S(2)}) copy-start(f32[128,256]{1,0:T(8,128)} %constant.16.clone.ends) | copy-start | bytes 393220
  2.7 44.3 %copy-start.6 = (f32[4,16,256]{2,1,0:T(8,128)S(1)}, f32[4,16,256]{2,1,0:T(8,128)}, u32[]{:S(2)}) copy-start(f32[4,16,256]{2,1,0:T(8,128)} %param.14) | copy-start | bytes 196612
  2.7 44.3 %copy-start.7 = (f32[64,40]{1,0:T(8,128)S(1)}, f32[64,40]{1,0:T(8,128)}, u32[]{:S(2)}) copy-start(f32[64,40]{1,0:T(8,128)} %constant.14.clone.along_x) | copy-start | bytes 30724
  4.2 2.1 %collective-permute-start = (f32[80,128]{1,0:T(8,128)S(1)}, f32[80,128]{1,0:T(8,128)S(1)}, u32[]{:S(2)}, u32[]{:S(2)}) collective-permute-start(f32[80,128]{1,0:T(8,128)S(1)} %get-tuple-element.11), channel_id=1, source_target_pairs={{0,1},{1,0},{2,3},{3,2},{4,5},{5,4},{6,7},{7,6},{8,9},{9,8},{10,11... | collective-permute-start | bytes 122888 | tf_op jit(solution)/shard_map/ppermute | solution.py:563

commit v2 on v1

--- a/solution.py
+++ b/solution.py
@@ -1,5 +1,3 @@
-import functools
-
 import jax
 import jax.numpy as jnp
 import numpy as np
@@ -18,9 +16,9 @@
 LINE_Y = 4
 PLANE = LINE_X * LINE_Y
 PACKED = 80
-SEND = 72
-FIRST = SEND + 16
-HIGHEST = lax.Precision.HIGHEST
+PAIRED = 72
+FIRST = 88
+SEND = 64
 step_rate = 0.15
 f32 = jnp.float32
 i32 = jnp.int32
@@ -96,6 +94,23 @@
     out[34] = np.where(lanes < 60, 1.0, 0.75)
     out[35] = 0.25
     return out.astype(np.float32), beside.astype(np.float32)
+
+
+def thirds(values):
+    high = values.astype(jnp.bfloat16)
+    rest = values - high.astype(f32)
+    middle = rest.astype(jnp.bfloat16)
+    return high, middle, (rest - middle.astype(f32)).astype(jnp.bfloat16)
+
+
+def dot_right(values, weights):
+    parts = [jnp.dot(part, weights, preferred_element_type=f32) for part in thirds(values)]
+    return parts[0] + (parts[1] + parts[2])
+
+
+def dot_left(weights, values):
+    parts = [jnp.dot(weights, part, preferred_element_type=f32) for part in thirds(values)]
+    return parts[0] + (parts[1] + parts[2])
 
 
 def position():
@@ -231,14 +246,6 @@
     def tile_row(y):
         return (y >> 3) * 16 + (y & 7)
 
-    def layers(y0):
-        for t in range(SIDE):
-            y = y0 - 1 + t
-            valid = True if 0 < t < SIDE - 1 else (y >= 0) & (y < 32)
-            yield t, jnp.clip(y, 0, 31), valid
-
-    weights = {0: (0.75, 0), 1: (0.25, 0), SIDE - 2: (0.25, 30), SIDE - 1: (0.75, 30)}
-
     def ends_of(u):
         low = 0.75 * u[:, 0:1] + 0.25 * u[:, 1:2]
         high = 0.75 * u[:, 9:10] + 0.25 * u[:, 8:9]
@@ -273,9 +280,7 @@
             for y in (low_y, high_y):
                 parts.append(brick[pl.ds(tile_row(y) + half * 8, 96, stride=64), :])
             sides.append(jnp.concatenate(parts, axis=0))
-        cells = jnp.dot(
-            jnp.concatenate(sides, axis=1), window, precision=HIGHEST, preferred_element_type=f32
-        )
+        cells = dot_right(jnp.concatenate(sides, axis=1), window.astype(jnp.bfloat16))
         inner = cells[:768].reshape(3, 32, B, 128)
         total = inner[0] * const[0:8, :][None]
         total = total + inner[1] * const[8:16, :][None]
@@ -285,27 +290,53 @@
             low = jnp.where(y0 > 0, const[24 + k : 25 + k, :], 0.0)
             high = jnp.where(y0 < 24, const[27 + k : 28 + k, :], 0.0)
             rows = rows + low * cells[768 + 32 * k : 800 + 32 * k] + high * cells[864 + 32 * k : 896 + 32 * k]
-        return rows
-
-    def edge_rows(x, y0, z_base, with_row):
-        flat = jnp.zeros((3, 128), f32)
+        flats = []
+        for x in (0, 31):
+            for k in range(3):
+                tile = jnp.where(lane < SIDE, cells[(k * 32 + x) * B : (k * 32 + x) * B + B], 0.0)
+                flat = jnp.sum(pltpu.roll(tile, SIDE, 1, stride=SIDE, stride_axis=0), axis=0, keepdims=True)
+                low = cells[768 + 32 * k + x : 769 + 32 * k + x]
+                high = cells[864 + 32 * k + x : 865 + 32 * k + x]
+                flat = flat + jnp.where((lane < SIDE) & (y0 > 0), low, 0.0)
+                flat = flat + pltpu.roll(jnp.where((lane < SIDE) & (y0 < 24), high, 0.0), 90, 1)
+                flats.append(flat)
+        return rows, flats
+
+    def edge_rows(x, y0, z_base):
+        start = (y0 >> 3) * 16
+        tiles = []
+        for k in range(3):
+            at = (k * 32 + x) * 64 + start
+            halves = [brick[pl.ds(pl.multiple_of(at + 8 * half, 8), 8), :] for half in range(2)]
+            tiles.append(jnp.concatenate(halves, axis=1))
+        u = pltpu.roll(jnp.concatenate(tiles, axis=0), (256 - z_base) & 255, 1)[:, :128]
+        at = z_base + lane
+        u = jnp.where((lane < SIDE) & (at >= 0) & (at < 256), u, 0.0)
+        low, high = ends_of(u)
+        flats, faces = [], []
+        for k in range(3):
+            tile = u[k * B : k * B + B]
+            flats.append(jnp.sum(pltpu.roll(tile, SIDE, 1, stride=SIDE, stride_axis=0), axis=0, keepdims=True))
+            tile = pltpu.roll(tile, 10 * k, 1) if k else tile
+            faces.append(tile + pltpu.roll(tile, 30, 1))
+        spread = jnp.where(lane < 60, jnp.concatenate(faces, axis=0), jnp.where(lane < 90, low, high))
+        total = jnp.sum(spread * const[0:24, :], axis=0, keepdims=True)
+        flat = jnp.where(sub3 == 0, flats[0], jnp.where(sub3 == 1, flats[1], flats[2]))
         row = jnp.zeros((3, 128), f32)
-        for t, y, valid in layers(y0):
-            u = shifted(x * 64 + tile_row(y), 3, 2048, z_base, valid)
+        for t, y, valid in ((0, y0 - 1, y0 > 0), (SIDE - 1, y0 + B, y0 < 24)):
+            u = shifted(x * 64 + tile_row(jnp.clip(y, 0, 31)), 3, 2048, z_base, valid)
             flat = flat + (pltpu.roll(u, 10 * t, 1) if t else u)
-            if with_row:
-                low, high = ends_of(u)
-                row = jnp.where(lane == 60 + 10 * sub3 + t, low, row)
-                row = jnp.where(lane == 90 + 10 * sub3 + t, high, row)
-                if t in weights:
-                    w, face = weights[t]
-                    spread = jnp.where(
-                        sub3 == 0,
-                        pltpu.roll(u, face, 1) if face else u,
-                        jnp.where(sub3 == 1, pltpu.roll(u, face + 10, 1), pltpu.roll(u, face + 20, 1)),
-                    )
-                    row = row + w * spread
-        return flat, jnp.sum(row, axis=0, keepdims=True)
+            low, high = ends_of(u)
+            row = jnp.where(lane == 60 + 10 * sub3 + t, low, row)
+            row = jnp.where(lane == 90 + 10 * sub3 + t, high, row)
+            face = 30 if t else 0
+            spread = jnp.where(
+                sub3 == 0,
+                pltpu.roll(u, face, 1) if face else u,
+                jnp.where(sub3 == 1, pltpu.roll(u, face + 10, 1), pltpu.roll(u, face + 20, 1)),
+            )
+            row = row + 0.75 * spread
+        return flat, total + jnp.sum(row, axis=0, keepdims=True)
 
     for dz in range(2):
         out = other_ref if dz else own_ref
@@ -331,14 +362,14 @@
                         out[48:80, :] += beside_rows(dy, z_base)
                     elif dx:
                         x, at = (0, 44) if dx == -1 else (31, 40)
-                        flat, row = edge_rows(x, y0, z_base, True)
+                        flat, row = edge_rows(x, y0, z_base)
                         out[at : at + 3, :] = 0.75 * flat
                         out[at + 3 : at + 4, :] = row
                     else:
-                        out[0:32, :] = all_rows(y0, z_base)
-                        for x, at in ((0, 32), (31, 35)):
-                            flat, _row = edge_rows(x, y0, z_base, False)
-                            out[at : at + 3, :] = 0.25 * flat
+                        rows, flats = all_rows(y0, z_base)
+                        out[0:32, :] = rows
+                        for i, flat in enumerate(flats):
+                            out[32 + i : 33 + i, :] = 0.25 * flat
                         if dz == 0:
                             start = (y0 >> 3) * 16 + (z0 >> 7) * 8
                             for n in range(96):
@@ -383,14 +414,14 @@
 
     for j in range(LINE_Z):
         gx, _, near_y, _, keep = read(j)
-        both = held[line_of(gx) + near_y, SEND:FIRST]
+        both = held[line_of(gx) + near_y, PAIRED:FIRST]
         rows[j * 32 : j * 32 + 16, :] = jnp.where(keep, both, 0.0)
         rows[j * 32 + 16 : j * 32 + 32, :] = jnp.where(keep, pltpu.roll(both, 64, 1), 0.0)
         for side in range(2):
             row = held[line_of(gx + (1 if side else -1)) + near_y, 32:40][6:7]
             at = LINE_Z * 32 + j * 2 + side
             rows[at : at + 1, :] = jnp.where(keep, pltpu.roll(row, 68, 1) if side else row, 0.0)
-    spread[...] = jnp.dot(rows[...], beside_ref[...], precision=HIGHEST, preferred_element_type=f32)
+    spread[...] = dot_right(rows[...], beside_ref[...])
 
     for j in range(LINE_Z):
         gx, gy, _, edge, _ = read(j)
@@ -403,20 +434,26 @@
 
         out[j, 0:32] = held[home_at, 0:32] + spread[j * 32 : j * 32 + 32, :]
         ends = held[home_at, 32:40]
-        for i, row in enumerate(flats(rows[j * 32 : j * 32 + 1, :]) + flats(rows[j * 32 + 31 : j * 32 + 32, :])):
-            ends = ends + jnp.where(sub == i, 0.25 * row, 0.0)
-        out[j, 32:40] = ends
         for side in range(2):
+            near = rows[j * 32 + 31 * side : j * 32 + 31 * side + 1, :]
             at = LINE_Z * 32 + j * 2 + side
-            added = [0.75 * row for row in flats(rows[at : at + 1, :])] + [spread[at : at + 1, :]]
             source = line_of(gx + (1 if side else -1)) + gy
+            pair = [held[source, 40 + (side * 2 + half) * 8 : 48 + (side * 2 + half) * 8] for half in range(2)]
+            ghosts = [ends[3 * side + k : 3 * side + k + 1] + 0.25 * row for k, row in enumerate(flats(near))]
+            pieces = (pair[0][6:7], pair[0][7:8], pair[1][6:7])
+            ghosts += [piece + 0.75 * row for piece, row in zip(pieces, flats(rows[at : at + 1, :]))]
+            ghosts.append(pair[1][7:8] + spread[at : at + 1, :])
+            tile = jnp.zeros((8, 128), f32)
+            for i, row in enumerate(ghosts):
+                tile = jnp.where(sub == i, row, tile)
             for half in range(2):
                 e = side * 2 + half
-                code = jnp.maximum(table[ROW_ROUTE, j * 4 + e] - 1, 0)
-                start = pl.multiple_of(40 + (code & 3) * 8, 8)
-                tile = held[source, 40 + e * 8 : 48 + e * 8]
-                tile = tile + jnp.where(sub == 6, added[2 * half], jnp.where(sub == 7, added[2 * half + 1], 0.0))
-                out[j, 40 + e * 8 : 48 + e * 8] = jnp.where(sub < 6, held[code >> 2, pl.ds(start, 8)], tile)
+                code = table[ROW_ROUTE, j * 4 + e] - 1
+                start = pl.multiple_of(40 + (jnp.maximum(code, 0) & 3) * 8, 8)
+                plane = held[jnp.maximum(code, 0) >> 2, pl.ds(start, 8)]
+                if half == 0:
+                    plane = jnp.where((sub < 6) & (code >= 0), plane, tile)
+                out[j, 32 + e * 8 : 40 + e * 8] = plane
 
 
 def update_kernel(
@@ -429,20 +466,17 @@
     at_home, at_low, at_high = gx & 7, (gx + 7) & 7, (gx + 1) & 7
     sub8 = lax.broadcasted_iota(i32, (8, 1), 0)
 
-    def piece_rows(at, tile, inside):
-        pair = [jnp.where(inside, rcv[at, tile + 8 * i : tile + 8 * i + 8], 0.0) for i in range(2)]
-        return pair[0][6:7], pair[0][7:8], pair[1][6:7], pair[1][7:8]
-
-    low = piece_rows(at_low, 40, gx > 0)
-    high = piece_rows(at_high, 56, gx < 31)
-    beyond = jnp.where(sub8 == 0, low[3], jnp.where(sub8 == 1, high[3], 0.0))
+    low = jnp.where(gx > 0, rcv[at_low, 32:40], 0.0)
+    high = jnp.where(gx < 31, rcv[at_high, 48:56], 0.0)
+    beyond = jnp.where(sub8 == 0, low[6:7], jnp.where(sub8 == 1, high[6:7], 0.0))
     body = jnp.concatenate([rcv[at_home, 0:32], beyond], axis=0)
-    dot = functools.partial(jnp.dot, precision=HIGHEST, preferred_element_type=f32)
-    sums[...] = dot(dot(along_x[...], body), faces[...])
-    flat = rcv[at_home, 32:40]
-    for i, row in enumerate(low[:3] + high[:3]):
-        flat = flat + jnp.where(sub8 == i, row, 0.0)
-    planes[...] = dot(flat, ends[...])
+    sums[...] = dot_right(dot_left(along_x[...], body), faces[...])
+    own = (rcv[at_home, 32:40], rcv[at_home, 48:56])
+    flat = jnp.zeros((8, 128), f32)
+    for side, other in enumerate((low, high)):
+        for k in range(3):
+            flat = jnp.where(sub8 == 3 * side + k, own[side][k : k + 1] + other[3 + k : 4 + k], flat)
+    planes[...] = dot_right(flat, ends[...])
     lane = lax.broadcasted_iota(i32, (1, F * F), 1)
     sub = lax.broadcasted_iota(i32, (F, 1), 0)
     lane_z = lane & (F - 1)
@@ -452,8 +486,8 @@
         box_start = pl.multiple_of(((word >> 1) & 3) * F, F)
         low_word = table[ROW_LOW, me * 4 + s]
         high_word = table[ROW_HIGH, me * 4 + s]
-        low_tile = rcv[low_word >> 4, pl.ds(pl.multiple_of(40 + ((low_word >> 2) & 3) * 8, 8), 8)]
-        high_tile = rcv[high_word >> 4, pl.ds(pl.multiple_of(40 + ((high_word >> 2) & 3) * 8, 8), 8)]
+        low_tile = rcv[low_word >> 4, pl.ds(pl.multiple_of(32 + ((low_word >> 2) & 3) * 8, 8), 8)]
+        high_tile = rcv[high_word >> 4, pl.ds(pl.multiple_of(32 + ((high_word >> 2) & 3) * 8, 8), 8)]
         visc = step_rate * visc_ref[s * F : s * F + F, :]
         for k in range(3):
             row = (k * SLOTS + s) * F
@@ -479,7 +513,7 @@
             advanced[at : at + F, :] = result
     for p in range(2):
         at = p * 96
-        pooled[p * 48 : p * 48 + 48, :] = dot(advanced[at : at + 48, :], pool[0]) + dot(
+        pooled[p * 48 : p * 48 + 48, :] = dot_right(advanced[at : at + 48, :], pool[0]) + dot_right(
             advanced[at + 48 : at + 96, :], pool[1]
         )
     means = pooled[pl.ds(0, 48, stride=2), :] + pooled[pl.ds(1, 48, stride=2), :]
@@ -546,6 +580,7 @@
     fine = fine_field.reshape(3 * SLOTS * F, F * F)
     tiles = coarse_field.reshape(3, 32, 4, 8, 2, 128).transpose(0, 1, 2, 4, 3, 5).reshape(6144, 128)
     pack_const, beside = map(jnp.asarray, pack_constants())
+    beside = beside.astype(jnp.bfloat16)
     table, own, other, planes, window = pl.pallas_call(
         pack_kernel,
         out_shape=(
@@ -592,7 +627,7 @@
             pltpu.VMEM((96, 128), f32),
         ],
         name="update", compiler_params=pltpu.CompilerParams(vmem_limit_bytes=16 << 20),
-    )(table, received, fine, viscosity.reshape(SLOTS * F, F * F), *map(jnp.asarray, constant_matrices()))
+    )(table, received, fine, viscosity.reshape(SLOTS * F, F * F), *(jnp.asarray(m, jnp.bfloat16) for m in constant_matrices()))
     held_means = lax.all_to_all(means, ("gx_0", "gy"), 0, 0)
     back = pl.pallas_call(
         return_kernel,

time: 77 us -> 75.3 us (0.978); the launches traced: 75.7 us -> 75.3 us
  Pallas kernels: 6.22 us -> 7.79 us
  blocking collectives: 64.6 us -> 63.4 us
  starting transfers between devices: 1.19 us -> 0.09 us
    all_to_all x1, blocking collectives: 19.8 us -> 18.6 us  [on_device(): received = lax.all_to_all(routed, 'gx_1', 0, 0)]
    ppermute x1, starting transfers between devices: 1.19 us -> 0.09 us  [on_device(): other = lax.ppermute(other, 'gz', [(0, 1), (1, 0)])]
    pallas_call x1, Pallas kernels: 0.62 us -> 1.57 us  [on_device(): pl.pallas_call(place_kernel, out_shape=shape(96, 32, 256), in_specs=[smem...]
    pallas_call x1, Pallas kernels: 1.45 us -> 2.38 us  [on_device(): pl.pallas_call(pack_kernel, out_shape=(shape(8, 128, dtype=i32), shape(PA...]
where the time goes in v2:
time: 75.3 us
  blocking collectives  63.4 us (84%)
  Pallas kernels  7.79 us (10%)
  local copies, waits for them, and re-layouts  2.02 us (3%)
  waiting for transfers between devices  1.21 us (2%)
  between operations  0.8 us (1%)
    all_to_all x1, blocking collectives, on_device(): held = lax.all_to_all(payload, ('gx_0', 'gy'), 0, 0)  19.8 us
    all_to_all x1, blocking collectives, on_device(): received = lax.all_to_all(routed, 'gx_1', 0, 0)  18.6 us
    all_to_all x1, blocking collectives, on_device(): held_means = lax.all_to_all(means, ('gx_0', 'gy'), 0, 0)  12.8 us
    all_to_all x1, blocking collectives, on_device(): returned = lax.all_to_all(back, 'gx_1', 0, 0)  12.2 us
    pallas_call x1, Pallas kernels, on_device(): pl.pallas_call(pack_kernel, out_shape=(shape(8, 128, dtype=i32), shape(PA...  2.38 us
    unnamed x25, local copies, waits for them, and re-layouts  2.02 us
    pallas_call x1, Pallas kernels, on_device(): pl.pallas_call(update_kernel, out_shape=(shape(3 * SLOTS * F, F * F), sha...  1.89 us
    pallas_call x1, Pallas kernels, on_device(): pl.pallas_call(place_kernel, out_shape=shape(96, 32, 256), in_specs=[smem...  1.57 us
  transfers between devices with their start and end apart: 1, of which 1 were waited for; matrix products, arithmetic and copies ran while one was open for 0% of the time, Pallas kernels for 0%

profile of v2, /device:TPU:2, one launch (start us, length us, event | category | flops | bytes accessed | tf_op | source)
XLA Modules:
  0.0 75.3 jit_solution(13147565389000102802)
XLA Ops:
  0.6 0.0 copy-start.7
  0.6 0.0 copy-start.1
  0.7 0.0 copy-start.9
  0.7 0.0 copy-start.11
  0.7 0.0 copy-start.10
  0.7 2.0 %copy.17 = f32[3,32,32,256]{3,2,1,0:T(8,128)S(1)} copy(f32[3,32,32,256]{3,2,1,0:T(8,128)} %param.12) | data formatting | bytes 6291456
  2.6 0.0 copy-start
  2.6 0.0 copy-start.6
  2.6 0.0 copy-done.7
  2.6 0.0 copy-done.1
  2.7 0.0 copy-done.9
  2.7 0.0 copy-done.11
  2.7 0.0 copy-done.10
  2.7 0.0 copy-start.2
  2.7 0.0 copy-start.3
  2.7 0.0 copy-start.4
  2.7 0.0 copy-start.5
  2.7 0.0 copy-start.8
  2.7 2.4 %pack.1 = (s32[8,128]{1,0:T(8,128)S(1)}, f32[80,128]{1,0:T(8,128)S(1)}, f32[80,128]{1,0:T(8,128)S(1)}, f32[32,128]{1,0:T(8,128)S(1)}, f32[768,128]{1,0:T(8,128)S(1)}) custom-call(s32[3,512]{1,0:T(4,128)S(1)} %bitcast.19, s32[1,512]{1,0:T(1,128)S(1)} %bitcast.21, s32[2,512]{1,0:T(2,128)S(1)} %bitcast.20, f32[192,256]{1,0:T(8,128)S(1)} %bitcast.16, ...), custom_call_target="tpu_custom_call" | custom-call | tf_op jit(solution)/shard_map/pack/pallas_call | solution.py:584
  5.1 0.1 collective-permute-start
  5.2 1.2 %collective-permute-done.other = f32[80,128]{1,0:T(8,128)S(1)} collective-permute-done((f32[80,128]{1,0:T(8,128)S(1)}, f32[80,128]{1,0:T(8,128)S(1)}, u32[]{:S(2)}, u32[]{:S(2)}) %collective-permute-start) | collective-permute-done | bytes 40992 | tf_op jit(solution)/shard_map/ppermute | solution.py:598
  6.4 0.1 join.1
  6.5 19.8 %all_to_all.20.held = f32[16,88,128]{2,1,0:T(8,128)S(1)} all-to-all(f32[16,88,128]{2,1,0:T(8,128)S(1)} %join.1), channel_id=1, replica_groups=mesh['gx_0'=4,'gx_1'=8,'gy'=4,'gz'=2] {'gx_0','gy'}, dimensions={0} | all-to-all | bytes 1441792 | tf_op jit(solution)/shard_map/all_to_all | solution.py:607
  26.3 0.0 copy-done.6
  26.3 1.1 %route.1 = f32[8,64,128]{2,1,0:T(8,128)S(1)} custom-call(s32[8,128]{1,0:T(8,128)S(1)} %get-tuple-element.9.table, f32[16,88,128]{2,1,0:T(8,128)S(1)} %all_to_all.20.held, bf16[128,128]{1,0:T(8,128)(2,1)S(1)} %copy-done.6), custom_call_target="tpu_custom_call" | custom-call | tf_op jit(solution)/shard_map/route/pallas_call | solution.py:608
  27.4 0.0 copy-done
  27.4 18.6 %all_to_all.21.rcv = f32[8,64,128]{2,1,0:T(8,128)S(1)} all-to-all(f32[8,64,128]{2,1,0:T(8,128)S(1)} %route.1), channel_id=1, replica_groups=mesh['gx_0'=4,'gx_1'=8,'gy'=4,'gz'=2] {'gx_1'}, dimensions={0} | all-to-all | bytes 524288 | tf_op jit(solution)/shard_map/all_to_all | solution.py:617
  46.0 0.0 copy-done.2
  46.0 0.0 copy-done.3
  46.0 0.0 copy-done.4
  46.0 0.0 copy-done.5
  46.0 0.0 copy-done.8
  46.0 1.9 %update.1 = (f32[192,256]{1,0:T(8,128)}, f32[16,48,128]{2,1,0:T(8,128)S(1)}) custom-call(s32[8,128]{1,0:T(8,128)S(1)} %get-tuple-element.9.table, f32[8,64,128]{2,1,0:T(8,128)S(1)} %all_to_all.21.rcv, f32[192,256]{1,0:T(8,128)S(1)} %bitcast.17, f32[64,256]{1,0:T(8,128)S(1)} %bitcast.18, bf16[64,40]{1,0:T(8,128)(2,1)S(1)} %copy-done.8, ...), custom_call_target="tpu_custom_call" | custom-call | tf_op jit(solution)/shard_map/update/pallas_call | solution.py:618
  47.9 12.8 %all_to_all.22.held = f32[16,48,128]{2,1,0:T(8,128)S(1)} all-to-all(f32[16,48,128]{2,1,0:T(8,128)S(1)} %get-tuple-element.14), channel_id=1, replica_groups=mesh['gx_0'=4,'gx_1'=8,'gy'=4,'gz'=2] {'gx_0','gy'}, dimensions={0} | all-to-all | bytes 786432 | tf_op jit(solution)/shard_map/all_to_all | solution.py:631
  60.7 0.8 %send_back.1 = f32[8,48,128]{2,1,0:T(8,128)S(1)} custom-call(s32[8,128]{1,0:T(8,128)S(1)} %get-tuple-element.9.table, f32[16,48,128]{2,1,0:T(8,128)S(1)} %all_to_all.22.held), custom_call_target="tpu_custom_call" | custom-call | tf_op jit(solution)/shard_map/send_back/pallas_call | solution.py:632
  61.5 12.2 %all_to_all.23.rcv = f32[8,48,128]{2,1,0:T(8,128)S(1)} all-to-all(f32[8,48,128]{2,1,0:T(8,128)S(1)} %send_back.1), channel_id=1, replica_groups=mesh['gx_0'=4,'gx_1'=8,'gy'=4,'gz'=2] {'gx_1'}, dimensions={0} | all-to-all | bytes 393216 | tf_op jit(solution)/shard_map/all_to_all | solution.py:639
  73.7 1.6 %place.1 = f32[96,32,256]{2,1,0:T(8,128)} custom-call(s32[8,128]{1,0:T(8,128)S(1)} %get-tuple-element.9.table, f32[8,48,128]{2,1,0:T(8,128)S(1)} %all_to_all.23.rcv, f32[768,128]{1,0:T(8,128)S(1)} %get-tuple-element.15.window, f32[96,32,256]{2,1,0:T(8,128)} %bitcast.14), custom_call_target="tpu_custom_call", output_to_operand_aliasing={{}: (3, {})} | custom-call | tf_op jit(solution)/shard_map/place/pallas_call | solution.py:640
Async XLA Ops:
  0.6 2.0 %copy-start.7 = (f32[40,128]{1,0:T(8,128)S(1)}, f32[40,128]{1,0:T(8,128)}, u32[]{:S(2)}) copy-start(f32[40,128]{1,0:T(8,128)} %constant.12.clone.const) | copy-start | bytes 61444
  0.6 2.0 %copy-start.1 = (f32[3,4,16,256]{3,2,1,0:T(8,128)S(1)}, f32[3,4,16,256]{3,2,1,0:T(8,128)}, u32[]{:S(2)}) copy-start(f32[3,4,16,256]{3,2,1,0:T(8,128)} %param.13) | copy-start | bytes 589828
  0.7 2.0 %copy-start.9 = (s32[512,3]{0,1:T(4,128)S(1)}, s32[512,3]{0,1:T(4,128)}, u32[]{:S(2)}) copy-start(s32[512,3]{0,1:T(4,128)} %param.15) | copy-start | bytes 18436
  0.7 2.0 %copy-start.11 = (s32[512]{0:T(512)S(1)}, s32[512]{0:T(512)}, u32[]{:S(2)}) copy-start(s32[512]{0:T(512)} %param.16) | copy-start | bytes 6148
  0.7 2.0 %copy-start.10 = (s32[512,2]{0,1:T(2,128)S(1)}, s32[512,2]{0,1:T(2,128)}, u32[]{:S(2)}) copy-start(s32[512,2]{0,1:T(2,128)} %param.17) | copy-start | bytes 12292
  2.6 24.8 %copy-start = (f32[3,32,32,256]{3,2,1,0:T(8,128)}, f32[3,32,32,256]{3,2,1,0:T(8,128)S(1)}, u32[]{:S(2)}) copy-start(f32[3,32,32,256]{3,2,1,0:T(8,128)S(1)} %copy.17) | copy-start | bytes 9437188
  2.6 23.7 %copy-start.6 = (bf16[128,128]{1,0:T(8,128)(2,1)S(1)}, bf16[128,128]{1,0:T(8,128)(2,1)}, u32[]{:S(2)}) copy-start(bf16[128,128]{1,0:T(8,128)(2,1)} %constant.20.beside_ref) | copy-start | bytes 98308
  2.7 43.3 %copy-start.2 = (bf16[128,768]{1,0:T(8,128)(2,1)S(1)}, bf16[128,768]{1,0:T(8,128)(2,1)}, u32[]{:S(2)}) copy-start(bf16[128,768]{1,0:T(8,128)(2,1)} %constant.15.clone.faces) | copy-start | bytes 589828
  2.7 43.3 %copy-start.3 = (bf16[2,256,128]{2,1,0:T(8,128)(2,1)S(1)}, bf16[2,256,128]{2,1,0:T(8,128)(2,1)}, u32[]{:S(2)}) copy-start(bf16[2,256,128]{2,1,0:T(8,128)(2,1)} %constant.17.clone.pool) | copy-start | bytes 393220
  2.7 43.3 %copy-start.4 = (f32[4,16,256]{2,1,0:T(8,128)S(1)}, f32[4,16,256]{2,1,0:T(8,128)}, u32[]{:S(2)}) copy-start(f32[4,16,256]{2,1,0:T(8,128)} %param.14) | copy-start | bytes 196612
  2.7 43.3 %copy-start.5 = (bf16[128,256]{1,0:T(8,128)(2,1)S(1)}, bf16[128,256]{1,0:T(8,128)(2,1)}, u32[]{:S(2)}) copy-start(bf16[128,256]{1,0:T(8,128)(2,1)} %constant.16.clone.ends) | copy-start | bytes 196612
  2.7 43.3 %copy-start.8 = (bf16[64,40]{1,0:T(8,128)(2,1)S(1)}, bf16[64,40]{1,0:T(8,128)(2,1)}, u32[]{:S(2)}) copy-start(bf16[64,40]{1,0:T(8,128)(2,1)} %constant.14.clone.along_x) | copy-start | bytes 15364
  5.1 1.3 %collective-permute-start = (f32[80,128]{1,0:T(8,128)S(1)}, f32[80,128]{1,0:T(8,128)S(1)}, u32[]{:S(2)}, u32[]{:S(2)}) collective-permute-start(f32[80,128]{1,0:T(8,128)S(1)} %get-tuple-element.11), channel_id=1, source_target_pairs={{0,1},{1,0},{2,3},{3,2},{4,5},{5,4},{6,7},{7,6},{8,9},{9,8},{10,11... | collective-permute-start | bytes 122888 | tf_op jit(solution)/shard_map/ppermute | solution.py:598

commit v3 on v2

--- a/solution.py
+++ b/solution.py
@@ -234,14 +234,22 @@
     lane = lax.broadcasted_iota(i32, (1, 128), 1)
     sub3 = lax.broadcasted_iota(i32, (3, 1), 0)
 
+    def from_second(z_base):
+        return z_base + ((lane - z_base) & 127) >= 128
+
+    def window_rows(at, second):
+        return jnp.where(second, brick[at(8)], brick[at(0)])
+
+    def to_front(rows, z_base, valid):
+        rows = pltpu.roll(rows, (256 - z_base) & 127, 1)
+        at = z_base + lane
+        return jnp.where((lane < SIDE) & (at >= 0) & (at < 256) & valid, rows, 0.0)
+
     def shifted(start, count, stride, z_base, valid):
-        rows = jnp.concatenate(
-            [brick[pl.ds(start + 8 * half, count, stride=stride), :] for half in range(2)], axis=1
+        rows = window_rows(
+            lambda tile: (pl.ds(start + tile, count, stride=stride), slice(None)), from_second(z_base)
         )
-        rows = pltpu.roll(rows, (256 - z_base) & 255, 1)[:, :128]
-        at = z_base + lane
-        keep = (lane < SIDE) & (at >= 0) & (at < 256) & valid
-        return jnp.where(keep, rows, 0.0)
+        return to_front(rows, z_base, valid)
 
     def tile_row(y):
         return (y >> 3) * 16 + (y & 7)
@@ -268,19 +276,25 @@
         return pltpu.roll(row, face, 1) if face else row
 
     def all_rows(y0, z_base):
-        offset = lax.broadcasted_iota(i32, (256, 1), 0) - z_base
-        offset = offset.astype(f32)
+        offset = (lax.broadcasted_iota(i32, (128, 1), 0) - z_base) & 127
+        offset = jnp.where((offset + z_base >= 0) & (offset + z_base < 256), offset, 500).astype(f32)
         window = jnp.where(offset == const[32:33, :], const[34:35, :], 0.0)
         window = window + jnp.where(offset == const[33:34, :], const[35:36, :], 0.0)
         start = (y0 >> 3) * 16
         low_y, high_y = jnp.maximum(y0 - 1, 0), jnp.minimum(y0 + B, 31)
-        sides = []
-        for half in range(2):
-            parts = [brick[pl.ds(pl.multiple_of(n * 64 + start + half * 8, 8), 8), :] for n in range(96)]
-            for y in (low_y, high_y):
-                parts.append(brick[pl.ds(tile_row(y) + half * 8, 96, stride=64), :])
-            sides.append(jnp.concatenate(parts, axis=0))
-        cells = dot_right(jnp.concatenate(sides, axis=1), window.astype(jnp.bfloat16))
+        tiles = from_second(z_base)
+        parts = []
+        for n in range(96):
+            first = n * 64 + start
+            parts.append(
+                window_rows(lambda tile, first=first: (pl.ds(pl.multiple_of(first + tile, 8), 8), slice(None)), tiles)
+            )
+        for y in (low_y, high_y):
+            first = tile_row(y)
+            parts.append(
+                window_rows(lambda tile, first=first: (pl.ds(first + tile, 96, stride=64), slice(None)), tiles)
+            )
+        cells = dot_right(jnp.concatenate(parts, axis=0), window.astype(jnp.bfloat16))
         inner = cells[:768].reshape(3, 32, B, 128)
         total = inner[0] * const[0:8, :][None]
         total = total + inner[1] * const[8:16, :][None]
@@ -304,14 +318,14 @@
 
     def edge_rows(x, y0, z_base):
         start = (y0 >> 3) * 16
-        tiles = []
-        for k in range(3):
-            at = (k * 32 + x) * 64 + start
-            halves = [brick[pl.ds(pl.multiple_of(at + 8 * half, 8), 8), :] for half in range(2)]
-            tiles.append(jnp.concatenate(halves, axis=1))
-        u = pltpu.roll(jnp.concatenate(tiles, axis=0), (256 - z_base) & 255, 1)[:, :128]
-        at = z_base + lane
-        u = jnp.where((lane < SIDE) & (at >= 0) & (at < 256), u, 0.0)
+        tiles = from_second(z_base)
+        rows = []
+        for k in range(3):
+            first = (k * 32 + x) * 64 + start
+            rows.append(
+                window_rows(lambda tile, first=first: (pl.ds(pl.multiple_of(first + tile, 8), 8), slice(None)), tiles)
+            )
+        u = to_front(jnp.concatenate(rows, axis=0), z_base, True)
         low, high = ends_of(u)
         flats, faces = [], []
         for k in range(3):
@@ -459,7 +473,7 @@
 def update_kernel(
     table, rcv, fine_ref, visc_ref, along_x, faces, ends, pool,
     fine_out, means_out,
-    sums, planes, advanced, pooled,
+    sums, planes, advanced, pooled, kept, sem,
 ):
     me = lax.axis_index("gx_1")
     gx = (jnp.maximum(table[ROW_HOME, me] - 1, 0) & 127) >> 2
@@ -508,9 +522,11 @@
             total = total + jnp.where(lane_z == 0, 0.0, pltpu.roll(cells, 1, 1))
             total = total + jnp.where(lane_z == F - 1, 0.0, pltpu.roll(cells, F * F - 1, 1))
             result = cells + visc * total
-            fine_out[row : row + F, :] = jnp.where(active, result, 0.0)
+            kept[row : row + F, :] = jnp.where(active, result, 0.0)
             at = s * 48 + k * F
             advanced[at : at + F, :] = result
+    store = pltpu.make_async_copy(kept, fine_out, sem)
+    store.start()
     for p in range(2):
         at = p * 96
         pooled[p * 48 : p * 48 + 48, :] = dot_right(advanced[at : at + 48, :], pool[0]) + dot_right(
@@ -519,6 +535,7 @@
     means = pooled[pl.ds(0, 48, stride=2), :] + pooled[pl.ds(1, 48, stride=2), :]
     for j in range(PLANE):
         means_out[j] = means
+    store.wait()
 
 
 def return_kernel(table, held, out):
@@ -544,20 +561,29 @@
         z0 = place & 255
         z_tile = pl.multiple_of((z0 >> 7) * 128, 128)
         z_in = z0 & 127
-        region = coarse_out.at[:, pl.ds(y0, 8), pl.ds(z_tile, 128)]
-        for i in range(SLOTS):
-            _, at, _, _ = split_slot(jnp.maximum(table[ROW_OWNER, me * 4 + i] - 1, 0))
-            for k in range(3):
+        lane = lax.broadcasted_iota(i32, (1, 128), 1)
+        owners = [split_slot(jnp.maximum(table[ROW_OWNER, me * 4 + i] - 1, 0))[1] for i in range(SLOTS)]
+        stores = []
+        for k in range(3):
+            for i in range(SLOTS):
                 start = ((i // 2) * 3 + k) * 8
-                values = rcv[at, start : start + 8]
+                values = rcv[owners[i], start : start + 8]
                 for b in range(B):
                     shift = (z_in + 256 - (b * B + 64 * (i % 2))) & 127
                     spread[pl.ds((k * 32 + i * B) * B + b, B, stride=B), :] = pltpu.roll(values, shift, 1)
-        lane = lax.broadcasted_iota(i32, (1, 128), 1)
-        spread[...] = jnp.where((lane >= z_in) & (lane < z_in + B), spread[...], window[...])
-        store = pltpu.make_async_copy(spread.reshape(96, 8, 128), region, sem)
-        store.start()
-        store.wait()
+            rows = pl.ds(k * 256, 256)
+            spread[rows, :] = jnp.where((lane >= z_in) & (lane < z_in + B), spread[rows, :], window[rows, :])
+            part = pl.ds(k * 32, 32)
+            stores.append(
+                pltpu.make_async_copy(
+                    spread.reshape(96, 8, 128).at[part],
+                    coarse_out.at[part, pl.ds(y0, 8), pl.ds(z_tile, 128)],
+                    sem.at[k],
+                )
+            )
+            stores[-1].start()
+        for store in stores:
+            store.wait()
 
 
 def vmem():
@@ -619,12 +645,14 @@
         update_kernel,
         out_shape=(shape(3 * SLOTS * F, F * F), shape(PLANE, 48, 128)),
         in_specs=[smem()] + [vmem()] * 7,
-        out_specs=(vmem(), vmem()),
+        out_specs=(anywhere(), vmem()),
         scratch_shapes=[
             pltpu.VMEM((64, 768), f32),
             pltpu.VMEM((8, 256), f32),
             pltpu.VMEM((192, 256), f32),
             pltpu.VMEM((96, 128), f32),
+            pltpu.VMEM((192, 256), f32),
+            pltpu.SemaphoreType.DMA(()),
         ],
         name="update", compiler_params=pltpu.CompilerParams(vmem_limit_bytes=16 << 20),
     )(table, received, fine, viscosity.reshape(SLOTS * F, F * F), *(jnp.asarray(m, jnp.bfloat16) for m in constant_matrices()))
@@ -643,7 +671,7 @@
         in_specs=[smem(), vmem(), vmem(), anywhere()],
         out_specs=anywhere(),
         input_output_aliases={3: 0},
-        scratch_shapes=[pltpu.VMEM((768, 128), f32), pltpu.SemaphoreType.DMA(())],
+        scratch_shapes=[pltpu.VMEM((768, 128), f32), pltpu.SemaphoreType.DMA((3,))],
         name="place", compiler_params=pltpu.CompilerParams(vmem_limit_bytes=8 << 20),
     )(table, returned, window, coarse_field.reshape(96, 32, 256))
     return fine_out.reshape(fine_field.shape), coarse_out.reshape(coarse_field.shape)

time: 75.3 us -> 75.2 us (level); the launches traced: 75.3 us -> 74 us
  Pallas kernels: 7.79 us -> 5.91 us
    pallas_call x1, Pallas kernels: 2.38 us -> 1.42 us  [on_device(): pl.pallas_call(pack_kernel, out_shape=(shape(8, 128, dtype=i32), shape(PA...]
    pallas_call x1, Pallas kernels: 1.57 us -> 0.64 us  [on_device(): pl.pallas_call(place_kernel, out_shape=shape(96, 32, 256), in_specs=[smem...]
where the time goes in v3:
time: 75.2 us; the launch traced here: 74 us
  blocking collectives  63.9 us (85%)
  Pallas kernels  5.91 us (8%)
  local copies, waits for them, and re-layouts  2.02 us (3%)
  waiting for transfers between devices  1.21 us (2%)
  between operations  0.81 us (1%)
    all_to_all x1, blocking collectives, on_device(): held = lax.all_to_all(payload, ('gx_0', 'gy'), 0, 0)  19.9 us
    all_to_all x1, blocking collectives, on_device(): received = lax.all_to_all(routed, 'gx_1', 0, 0)  19.1 us
    all_to_all x1, blocking collectives, on_device(): held_means = lax.all_to_all(means, ('gx_0', 'gy'), 0, 0)  12.8 us
    all_to_all x1, blocking collectives, on_device(): returned = lax.all_to_all(back, 'gx_1', 0, 0)  12.2 us
    unnamed x25, local copies, waits for them, and re-layouts  2.02 us
    pallas_call x1, Pallas kernels, on_device(): pl.pallas_call(update_kernel, out_shape=(shape(3 * SLOTS * F, F * F), sha...  1.9 us
  transfers between devices with their start and end apart: 1, of which 1 were waited for; matrix products, arithmetic and copies ran while one was open for 0% of the time, Pallas kernels for 0%

profile of v3, /device:TPU:2, one launch (start us, length us, event | category | flops | bytes accessed | tf_op | source)
XLA Modules:
  0.0 74.0 jit_solution(12977950944816081385)
XLA Ops:
  0.6 0.0 copy-start.7
  0.6 0.0 copy-start.1
  0.7 0.0 copy-start.9
  0.7 0.0 copy-start.11
  0.7 0.0 copy-start.10
  0.7 2.0 %copy.17 = f32[3,32,32,256]{3,2,1,0:T(8,128)S(1)} copy(f32[3,32,32,256]{3,2,1,0:T(8,128)} %param.12) | data formatting | bytes 6291456
  2.6 0.0 copy-start
  2.6 0.0 copy-start.6
  2.6 0.0 copy-done.7
  2.6 0.0 copy-done.1
  2.7 0.0 copy-done.9
  2.7 0.0 copy-done.11
  2.7 0.0 copy-done.10
  2.7 0.0 copy-start.2
  2.7 0.0 copy-start.3
  2.7 0.0 copy-start.4
  2.7 0.0 copy-start.5
  2.7 0.0 copy-start.8
  2.7 1.4 %pack.1 = (s32[8,128]{1,0:T(8,128)S(1)}, f32[80,128]{1,0:T(8,128)S(1)}, f32[80,128]{1,0:T(8,128)S(1)}, f32[32,128]{1,0:T(8,128)S(1)}, f32[768,128]{1,0:T(8,128)S(1)}) custom-call(s32[3,512]{1,0:T(4,128)S(1)} %bitcast.19, s32[1,512]{1,0:T(1,128)S(1)} %bitcast.21, s32[2,512]{1,0:T(2,128)S(1)} %bitcast.20, f32[192,256]{1,0:T(8,128)S(1)} %bitcast.16, ...), custom_call_target="tpu_custom_call" | custom-call | tf_op jit(solution)/shard_map/pack/pallas_call | solution.py:610
  4.2 0.1 collective-permute-start
  4.3 1.2 %collective-permute-done.other = f32[80,128]{1,0:T(8,128)S(1)} collective-permute-done((f32[80,128]{1,0:T(8,128)S(1)}, f32[80,128]{1,0:T(8,128)S(1)}, u32[]{:S(2)}, u32[]{:S(2)}) %collective-permute-start) | collective-permute-done | bytes 40992 | tf_op jit(solution)/shard_map/ppermute | solution.py:624
  5.5 0.1 join.1
  5.6 19.9 %all_to_all.20.held = f32[16,88,128]{2,1,0:T(8,128)S(1)} all-to-all(f32[16,88,128]{2,1,0:T(8,128)S(1)} %join.1), channel_id=1, replica_groups=mesh['gx_0'=4,'gx_1'=8,'gy'=4,'gz'=2] {'gx_0','gy'}, dimensions={0} | all-to-all | bytes 1441792 | tf_op jit(solution)/shard_map/all_to_all | solution.py:633
  25.4 0.0 copy-done.6
  25.4 1.1 %route.1 = f32[8,64,128]{2,1,0:T(8,128)S(1)} custom-call(s32[8,128]{1,0:T(8,128)S(1)} %get-tuple-element.9.table, f32[16,88,128]{2,1,0:T(8,128)S(1)} %all_to_all.20.held, bf16[128,128]{1,0:T(8,128)(2,1)S(1)} %copy-done.6), custom_call_target="tpu_custom_call" | custom-call | tf_op jit(solution)/shard_map/route/pallas_call | solution.py:634
  26.5 0.0 copy-done
  26.5 19.1 %all_to_all.21.rcv = f32[8,64,128]{2,1,0:T(8,128)S(1)} all-to-all(f32[8,64,128]{2,1,0:T(8,128)S(1)} %route.1), channel_id=1, replica_groups=mesh['gx_0'=4,'gx_1'=8,'gy'=4,'gz'=2] {'gx_1'}, dimensions={0} | all-to-all | bytes 524288 | tf_op jit(solution)/shard_map/all_to_all | solution.py:643
  45.6 0.0 copy-done.2
  45.6 0.0 copy-done.3
  45.6 0.0 copy-done.4
  45.6 0.0 copy-done.5
  45.6 0.0 copy-done.8
  45.6 1.9 %update.1 = (f32[192,256]{1,0:T(8,128)}, f32[16,48,128]{2,1,0:T(8,128)S(1)}) custom-call(s32[8,128]{1,0:T(8,128)S(1)} %get-tuple-element.9.table, f32[8,64,128]{2,1,0:T(8,128)S(1)} %all_to_all.21.rcv, f32[192,256]{1,0:T(8,128)S(1)} %bitcast.17, f32[64,256]{1,0:T(8,128)S(1)} %bitcast.18, bf16[64,40]{1,0:T(8,128)(2,1)S(1)} %copy-done.8, ...), custom_call_target="tpu_custom_call" | custom-call | tf_op jit(solution)/shard_map/update/pallas_call | solution.py:644
  47.5 12.8 %all_to_all.22.held = f32[16,48,128]{2,1,0:T(8,128)S(1)} all-to-all(f32[16,48,128]{2,1,0:T(8,128)S(1)} %get-tuple-element.14), channel_id=1, replica_groups=mesh['gx_0'=4,'gx_1'=8,'gy'=4,'gz'=2] {'gx_0','gy'}, dimensions={0} | all-to-all | bytes 786432 | tf_op jit(solution)/shard_map/all_to_all | solution.py:659
  60.4 0.8 %send_back.1 = f32[8,48,128]{2,1,0:T(8,128)S(1)} custom-call(s32[8,128]{1,0:T(8,128)S(1)} %get-tuple-element.9.table, f32[16,48,128]{2,1,0:T(8,128)S(1)} %all_to_all.22.held), custom_call_target="tpu_custom_call" | custom-call | tf_op jit(solution)/shard_map/send_back/pallas_call | solution.py:660
  61.2 12.2 %all_to_all.23.rcv = f32[8,48,128]{2,1,0:T(8,128)S(1)} all-to-all(f32[8,48,128]{2,1,0:T(8,128)S(1)} %send_back.1), channel_id=1, replica_groups=mesh['gx_0'=4,'gx_1'=8,'gy'=4,'gz'=2] {'gx_1'}, dimensions={0} | all-to-all | bytes 393216 | tf_op jit(solution)/shard_map/all_to_all | solution.py:667
  73.4 0.6 place.1
Async XLA Ops:
  0.6 2.0 %copy-start.7 = (f32[40,128]{1,0:T(8,128)S(1)}, f32[40,128]{1,0:T(8,128)}, u32[]{:S(2)}) copy-start(f32[40,128]{1,0:T(8,128)} %constant.12.clone.const) | copy-start | bytes 61444
  0.6 2.0 %copy-start.1 = (f32[3,4,16,256]{3,2,1,0:T(8,128)S(1)}, f32[3,4,16,256]{3,2,1,0:T(8,128)}, u32[]{:S(2)}) copy-start(f32[3,4,16,256]{3,2,1,0:T(8,128)} %param.13) | copy-start | bytes 589828
  0.7 2.0 %copy-start.9 = (s32[512,3]{0,1:T(4,128)S(1)}, s32[512,3]{0,1:T(4,128)}, u32[]{:S(2)}) copy-start(s32[512,3]{0,1:T(4,128)} %param.15) | copy-start | bytes 18436
  0.7 2.0 %copy-start.11 = (s32[512]{0:T(512)S(1)}, s32[512]{0:T(512)}, u32[]{:S(2)}) copy-start(s32[512]{0:T(512)} %param.16) | copy-start | bytes 6148
  0.7 2.0 %copy-start.10 = (s32[512,2]{0,1:T(2,128)S(1)}, s32[512,2]{0,1:T(2,128)}, u32[]{:S(2)}) copy-start(s32[512,2]{0,1:T(2,128)} %param.17) | copy-start | bytes 12292
  2.6 23.8 %copy-start = (f32[3,32,32,256]{3,2,1,0:T(8,128)}, f32[3,32,32,256]{3,2,1,0:T(8,128)S(1)}, u32[]{:S(2)}) copy-start(f32[3,32,32,256]{3,2,1,0:T(8,128)S(1)} %copy.17) | copy-start | bytes 9437188
  2.6 22.8 %copy-start.6 = (bf16[128,128]{1,0:T(8,128)(2,1)S(1)}, bf16[128,128]{1,0:T(8,128)(2,1)}, u32[]{:S(2)}) copy-start(bf16[128,128]{1,0:T(8,128)(2,1)} %constant.20.beside_ref) | copy-start | bytes 98308
  2.7 42.9 %copy-start.2 = (bf16[128,768]{1,0:T(8,128)(2,1)S(1)}, bf16[128,768]{1,0:T(8,128)(2,1)}, u32[]{:S(2)}) copy-start(bf16[128,768]{1,0:T(8,128)(2,1)} %constant.15.clone.faces) | copy-start | bytes 589828
  2.7 42.9 %copy-start.3 = (bf16[2,256,128]{2,1,0:T(8,128)(2,1)S(1)}, bf16[2,256,128]{2,1,0:T(8,128)(2,1)}, u32[]{:S(2)}) copy-start(bf16[2,256,128]{2,1,0:T(8,128)(2,1)} %constant.17.clone.pool) | copy-start | bytes 393220
  2.7 42.9 %copy-start.4 = (f32[4,16,256]{2,1,0:T(8,128)S(1)}, f32[4,16,256]{2,1,0:T(8,128)}, u32[]{:S(2)}) copy-start(f32[4,16,256]{2,1,0:T(8,128)} %param.14) | copy-start | bytes 196612
  2.7 42.9 %copy-start.5 = (bf16[128,256]{1,0:T(8,128)(2,1)S(1)}, bf16[128,256]{1,0:T(8,128)(2,1)}, u32[]{:S(2)}) copy-start(bf16[128,256]{1,0:T(8,128)(2,1)} %constant.16.clone.ends) | copy-start | bytes 196612
  2.7 42.9 %copy-start.8 = (bf16[64,40]{1,0:T(8,128)(2,1)S(1)}, bf16[64,40]{1,0:T(8,128)(2,1)}, u32[]{:S(2)}) copy-start(bf16[64,40]{1,0:T(8,128)(2,1)} %constant.14.clone.along_x) | copy-start | bytes 15364
  4.2 1.3 %collective-permute-start = (f32[80,128]{1,0:T(8,128)S(1)}, f32[80,128]{1,0:T(8,128)S(1)}, u32[]{:S(2)}, u32[]{:S(2)}) collective-permute-start(f32[80,128]{1,0:T(8,128)S(1)} %get-tuple-element.11), channel_id=1, source_target_pairs={{0,1},{1,0},{2,3},{3,2},{4,5},{5,4},{6,7},{7,6},{8,9},{9,8},{10,11... | collective-permute-start | bytes 122888 | tf_op jit(solution)/shard_map/ppermute | solution.py:624

commit v4 on v3

--- a/solution.py
+++ b/solution.py
@@ -18,7 +18,7 @@
 PACKED = 80
 PAIRED = 72
 FIRST = 88
-SEND = 64
+SEND = 56
 step_rate = 0.15
 f32 = jnp.float32
 i32 = jnp.int32
@@ -181,7 +181,7 @@
             here, there = 2 + after(my_mask, my_box), before(near_mask, near_box)
         target = jnp.where(same_j & ((lanes & 3) == here) & outer, 1.0, 0.0)
         plane = (device >> 6) * LINE_Y + ((device >> 1) & 3)
-        code = (plane * 4 + there + 1).astype(f32)
+        code = (plane * 4 + there + near_box * 64 + 1).astype(f32)
         route_row = route_row + jnp.sum(target * code, axis=0, keepdims=True)
         sends_row = sends_row + jnp.sum(target * ((sub & 3) + 1).astype(f32), axis=0, keepdims=True)
         word = jnp.where(outer, 2 + here * 4 + ((device >> 3) & 7) * 16, 1 + ((slot - 1) & 3) * 4)
@@ -461,13 +461,18 @@
             for i, row in enumerate(ghosts):
                 tile = jnp.where(sub == i, row, tile)
             for half in range(2):
-                e = side * 2 + half
-                code = table[ROW_ROUTE, j * 4 + e] - 1
-                start = pl.multiple_of(40 + (jnp.maximum(code, 0) & 3) * 8, 8)
-                plane = held[jnp.maximum(code, 0) >> 2, pl.ds(start, 8)]
+                code = table[ROW_ROUTE, j * 4 + side * 2 + half] - 1
+                used = code >= 0
+                code = jnp.maximum(code, 0)
+                plane = held[(code >> 2) & 15, pl.ds(pl.multiple_of(40 + (code & 3) * 8, 8), 8)]
                 if half == 0:
-                    plane = jnp.where((sub < 6) & (code >= 0), plane, tile)
-                out[j, 32 + e * 8 : 40 + e * 8] = plane
+                    out[j, 32 + side * 8 : 40 + side * 8] = jnp.where((sub < 6) & used, plane, tile)
+                elif side == 1:
+                    out[j, 48:56] = plane
+                else:
+                    between = pl.ds(pl.multiple_of((code >> 6) * 8, 8), 8)
+                    inner = (sub >= 1) & (sub <= 6) & used
+                    out[j, between] = jnp.where(inner, pltpu.roll(plane, 1, 0), out[j, between])
 
 
 def update_kernel(
@@ -481,11 +486,11 @@
     sub8 = lax.broadcasted_iota(i32, (8, 1), 0)
 
     low = jnp.where(gx > 0, rcv[at_low, 32:40], 0.0)
-    high = jnp.where(gx < 31, rcv[at_high, 48:56], 0.0)
+    high = jnp.where(gx < 31, rcv[at_high, 40:48], 0.0)
     beyond = jnp.where(sub8 == 0, low[6:7], jnp.where(sub8 == 1, high[6:7], 0.0))
     body = jnp.concatenate([rcv[at_home, 0:32], beyond], axis=0)
     sums[...] = dot_right(dot_left(along_x[...], body), faces[...])
-    own = (rcv[at_home, 32:40], rcv[at_home, 48:56])
+    own = (rcv[at_home, 32:40], rcv[at_home, 40:48])
     flat = jnp.zeros((8, 128), f32)
     for side, other in enumerate((low, high)):
         for k in range(3):
@@ -500,8 +505,12 @@
         box_start = pl.multiple_of(((word >> 1) & 3) * F, F)
         low_word = table[ROW_LOW, me * 4 + s]
         high_word = table[ROW_HIGH, me * 4 + s]
-        low_tile = rcv[low_word >> 4, pl.ds(pl.multiple_of(32 + ((low_word >> 2) & 3) * 8, 8), 8)]
-        high_tile = rcv[high_word >> 4, pl.ds(pl.multiple_of(32 + ((high_word >> 2) & 3) * 8, 8), 8)]
+        second = (low_word & 7) == 6
+        low_at = jnp.where(second, (((word >> 1) & 3) + 3) & 3, 4) * 8
+        low_tile = rcv[low_word >> 4, pl.ds(pl.multiple_of(low_at, 8), 8)]
+        low_tile = jnp.where(second, pltpu.roll(low_tile, 7, 0), low_tile)
+        high_at = jnp.where((high_word & 15) == 14, 48, 40)
+        high_tile = rcv[high_word >> 4, pl.ds(pl.multiple_of(high_at, 8), 8)]
         visc = step_rate * visc_ref[s * F : s * F + F, :]
         for k in range(3):
             row = (k * SLOTS + s) * F

time: 75.2 us -> 74.4 us (0.989); the launches traced: 74 us -> 74 us
  Pallas kernels: 5.91 us -> 7.67 us
  blocking collectives: 63.9 us -> 62.2 us
    all_to_all x1, blocking collectives: 19.9 us -> 18.9 us  [on_device(): held = lax.all_to_all(payload, ('gx_0', 'gy'), 0, 0)]
    pallas_call x1, Pallas kernels: 1.42 us -> 2.29 us  [on_device(): pl.pallas_call(pack_kernel, out_shape=(shape(8, 128, dtype=i32), shape(PA...]
    pallas_call x1, Pallas kernels: 0.64 us -> 1.5 us  [on_device(): pl.pallas_call(place_kernel, out_shape=shape(96, 32, 256), in_specs=[smem...]
where the time goes in v4:
time: 74.4 us; the launch traced here: 74 us
  blocking collectives  62.2 us (84%)
  Pallas kernels  7.67 us (10%)
  local copies, waits for them, and re-layouts  2.02 us (3%)
  waiting for transfers between devices  1.21 us (2%)
  between operations  0.81 us (1%)
    all_to_all x1, blocking collectives, on_device(): held = lax.all_to_all(payload, ('gx_0', 'gy'), 0, 0)  18.9 us
    all_to_all x1, blocking collectives, on_device(): received = lax.all_to_all(routed, 'gx_1', 0, 0)  18.7 us
    all_to_all x1, blocking collectives, on_device(): held_means = lax.all_to_all(means, ('gx_0', 'gy'), 0, 0)  12.5 us
    all_to_all x1, blocking collectives, on_device(): returned = lax.all_to_all(back, 'gx_1', 0, 0)  12.2 us
    pallas_call x1, Pallas kernels, on_device(): pl.pallas_call(pack_kernel, out_shape=(shape(8, 128, dtype=i32), shape(PA...  2.29 us
    unnamed x25, local copies, waits for them, and re-layouts  2.02 us
    pallas_call x1, Pallas kernels, on_device(): pl.pallas_call(update_kernel, out_shape=(shape(3 * SLOTS * F, F * F), sha...  1.9 us
    pallas_call x1, Pallas kernels, on_device(): pl.pallas_call(place_kernel, out_shape=shape(96, 32, 256), in_specs=[smem...  1.5 us
  transfers between devices with their start and end apart: 1, of which 1 were waited for; matrix products, arithmetic and copies ran while one was open for 0% of the time, Pallas kernels for 0%

profile of v4, /device:TPU:2, one launch (start us, length us, event | category | flops | bytes accessed | tf_op | source)
XLA Modules:
  0.0 74.0 jit_solution(1763753512920863356)
XLA Ops:
  0.6 0.0 copy-start.7
  0.6 0.0 copy-start.1
  0.7 0.0 copy-start.9
  0.7 0.0 copy-start.11
  0.7 0.0 copy-start.10
  0.7 2.0 %copy.17 = f32[3,32,32,256]{3,2,1,0:T(8,128)S(1)} copy(f32[3,32,32,256]{3,2,1,0:T(8,128)} %param.12) | data formatting | bytes 6291456
  2.6 0.0 copy-start
  2.6 0.0 copy-start.6
  2.6 0.0 copy-done.7
  2.6 0.0 copy-done.1
  2.7 0.0 copy-done.9
  2.7 0.0 copy-done.11
  2.7 0.0 copy-done.10
  2.7 0.0 copy-start.2
  2.7 0.0 copy-start.3
  2.7 0.0 copy-start.4
  2.7 0.0 copy-start.5
  2.7 0.0 copy-start.8
  2.7 2.3 %pack.1 = (s32[8,128]{1,0:T(8,128)S(1)}, f32[80,128]{1,0:T(8,128)S(1)}, f32[80,128]{1,0:T(8,128)S(1)}, f32[32,128]{1,0:T(8,128)S(1)}, f32[768,128]{1,0:T(8,128)S(1)}) custom-call(s32[3,512]{1,0:T(4,128)S(1)} %bitcast.19, s32[1,512]{1,0:T(1,128)S(1)} %bitcast.21, s32[2,512]{1,0:T(2,128)S(1)} %bitcast.20, f32[192,256]{1,0:T(8,128)S(1)} %bitcast.16, ...), custom_call_target="tpu_custom_call" | custom-call | tf_op jit(solution)/shard_map/pack/pallas_call | solution.py:619
  5.0 0.1 collective-permute-start
  5.1 1.2 %collective-permute-done.other = f32[80,128]{1,0:T(8,128)S(1)} collective-permute-done((f32[80,128]{1,0:T(8,128)S(1)}, f32[80,128]{1,0:T(8,128)S(1)}, u32[]{:S(2)}, u32[]{:S(2)}) %collective-permute-start) | collective-permute-done | bytes 40992 | tf_op jit(solution)/shard_map/ppermute | solution.py:633
  6.4 0.1 join.1
  6.4 18.9 %all_to_all.20.held = f32[16,88,128]{2,1,0:T(8,128)S(1)} all-to-all(f32[16,88,128]{2,1,0:T(8,128)S(1)} %join.1), channel_id=1, replica_groups=mesh['gx_0'=4,'gx_1'=8,'gy'=4,'gz'=2] {'gx_0','gy'}, dimensions={0} | all-to-all | bytes 1441792 | tf_op jit(solution)/shard_map/all_to_all | solution.py:642
  25.3 0.0 copy-done.6
  25.3 1.1 %route.1 = f32[8,56,128]{2,1,0:T(8,128)S(1)} custom-call(s32[8,128]{1,0:T(8,128)S(1)} %get-tuple-element.9.table, f32[16,88,128]{2,1,0:T(8,128)S(1)} %all_to_all.20.held, bf16[128,128]{1,0:T(8,128)(2,1)S(1)} %copy-done.6), custom_call_target="tpu_custom_call" | custom-call | tf_op jit(solution)/shard_map/route/pallas_call | solution.py:643
  26.4 0.0 copy-done
  26.4 18.7 %all_to_all.21.rcv = f32[8,56,128]{2,1,0:T(8,128)S(1)} all-to-all(f32[8,56,128]{2,1,0:T(8,128)S(1)} %route.1), channel_id=1, replica_groups=mesh['gx_0'=4,'gx_1'=8,'gy'=4,'gz'=2] {'gx_1'}, dimensions={0} | all-to-all | bytes 458752 | tf_op jit(solution)/shard_map/all_to_all | solution.py:652
  45.1 0.0 copy-done.2
  45.1 0.0 copy-done.3
  45.1 0.0 copy-done.4
  45.1 0.0 copy-done.5
  45.1 0.0 copy-done.8
  45.1 1.9 %update.1 = (f32[192,256]{1,0:T(8,128)}, f32[16,48,128]{2,1,0:T(8,128)S(1)}) custom-call(s32[8,128]{1,0:T(8,128)S(1)} %get-tuple-element.9.table, f32[8,56,128]{2,1,0:T(8,128)S(1)} %all_to_all.21.rcv, f32[192,256]{1,0:T(8,128)S(1)} %bitcast.17, f32[64,256]{1,0:T(8,128)S(1)} %bitcast.18, bf16[64,40]{1,0:T(8,128)(2,1)S(1)} %copy-done.8, ...), custom_call_target="tpu_custom_call" | custom-call | tf_op jit(solution)/shard_map/update/pallas_call | solution.py:653
  47.0 12.5 %all_to_all.22.held = f32[16,48,128]{2,1,0:T(8,128)S(1)} all-to-all(f32[16,48,128]{2,1,0:T(8,128)S(1)} %get-tuple-element.14), channel_id=1, replica_groups=mesh['gx_0'=4,'gx_1'=8,'gy'=4,'gz'=2] {'gx_0','gy'}, dimensions={0} | all-to-all | bytes 786432 | tf_op jit(solution)/shard_map/all_to_all | solution.py:668
  59.5 0.8 %send_back.1 = f32[8,48,128]{2,1,0:T(8,128)S(1)} custom-call(s32[8,128]{1,0:T(8,128)S(1)} %get-tuple-element.9.table, f32[16,48,128]{2,1,0:T(8,128)S(1)} %all_to_all.22.held), custom_call_target="tpu_custom_call" | custom-call | tf_op jit(solution)/shard_map/send_back/pallas_call | solution.py:669
  60.3 12.2 %all_to_all.23.rcv = f32[8,48,128]{2,1,0:T(8,128)S(1)} all-to-all(f32[8,48,128]{2,1,0:T(8,128)S(1)} %send_back.1), channel_id=1, replica_groups=mesh['gx_0'=4,'gx_1'=8,'gy'=4,'gz'=2] {'gx_1'}, dimensions={0} | all-to-all | bytes 393216 | tf_op jit(solution)/shard_map/all_to_all | solution.py:676
  72.5 1.5 %place.1 = f32[96,32,256]{2,1,0:T(8,128)} custom-call(s32[8,128]{1,0:T(8,128)S(1)} %get-tuple-element.9.table, f32[8,48,128]{2,1,0:T(8,128)S(1)} %all_to_all.23.rcv, f32[768,128]{1,0:T(8,128)S(1)} %get-tuple-element.15.window, f32[96,32,256]{2,1,0:T(8,128)} %bitcast.14), custom_call_target="tpu_custom_call", output_to_operand_aliasing={{}: (3, {})} | custom-call | tf_op jit(solution)/shard_map/place/pallas_call | solution.py:677
Async XLA Ops:
  0.6 2.0 %copy-start.7 = (f32[40,128]{1,0:T(8,128)S(1)}, f32[40,128]{1,0:T(8,128)}, u32[]{:S(2)}) copy-start(f32[40,128]{1,0:T(8,128)} %constant.12.clone.const) | copy-start | bytes 61444
  0.6 2.0 %copy-start.1 = (f32[3,4,16,256]{3,2,1,0:T(8,128)S(1)}, f32[3,4,16,256]{3,2,1,0:T(8,128)}, u32[]{:S(2)}) copy-start(f32[3,4,16,256]{3,2,1,0:T(8,128)} %param.13) | copy-start | bytes 589828
  0.7 2.0 %copy-start.9 = (s32[512,3]{0,1:T(4,128)S(1)}, s32[512,3]{0,1:T(4,128)}, u32[]{:S(2)}) copy-start(s32[512,3]{0,1:T(4,128)} %param.15) | copy-start | bytes 18436
  0.7 2.0 %copy-start.11 = (s32[512]{0:T(512)S(1)}, s32[512]{0:T(512)}, u32[]{:S(2)}) copy-start(s32[512]{0:T(512)} %param.16) | copy-start | bytes 6148
  0.7 2.0 %copy-start.10 = (s32[512,2]{0,1:T(2,128)S(1)}, s32[512,2]{0,1:T(2,128)}, u32[]{:S(2)}) copy-start(s32[512,2]{0,1:T(2,128)} %param.17) | copy-start | bytes 12292
  2.6 23.7 %copy-start = (f32[3,32,32,256]{3,2,1,0:T(8,128)}, f32[3,32,32,256]{3,2,1,0:T(8,128)S(1)}, u32[]{:S(2)}) copy-start(f32[3,32,32,256]{3,2,1,0:T(8,128)S(1)} %copy.17) | copy-start | bytes 9437188
  2.6 22.7 %copy-start.6 = (bf16[128,128]{1,0:T(8,128)(2,1)S(1)}, bf16[128,128]{1,0:T(8,128)(2,1)}, u32[]{:S(2)}) copy-start(bf16[128,128]{1,0:T(8,128)(2,1)} %constant.20.beside_ref) | copy-start | bytes 98308
  2.7 42.4 %copy-start.2 = (bf16[128,768]{1,0:T(8,128)(2,1)S(1)}, bf16[128,768]{1,0:T(8,128)(2,1)}, u32[]{:S(2)}) copy-start(bf16[128,768]{1,0:T(8,128)(2,1)} %constant.15.clone.faces) | copy-start | bytes 589828
  2.7 42.4 %copy-start.3 = (bf16[2,256,128]{2,1,0:T(8,128)(2,1)S(1)}, bf16[2,256,128]{2,1,0:T(8,128)(2,1)}, u32[]{:S(2)}) copy-start(bf16[2,256,128]{2,1,0:T(8,128)(2,1)} %constant.17.clone.pool) | copy-start | bytes 393220
  2.7 42.4 %copy-start.4 = (f32[4,16,256]{2,1,0:T(8,128)S(1)}, f32[4,16,256]{2,1,0:T(8,128)}, u32[]{:S(2)}) copy-start(f32[4,16,256]{2,1,0:T(8,128)} %param.14) | copy-start | bytes 196612
  2.7 42.4 %copy-start.5 = (bf16[128,256]{1,0:T(8,128)(2,1)S(1)}, bf16[128,256]{1,0:T(8,128)(2,1)}, u32[]{:S(2)}) copy-start(bf16[128,256]{1,0:T(8,128)(2,1)} %constant.16.clone.ends) | copy-start | bytes 196612
  2.7 42.4 %copy-start.8 = (bf16[64,40]{1,0:T(8,128)(2,1)S(1)}, bf16[64,40]{1,0:T(8,128)(2,1)}, u32[]{:S(2)}) copy-start(bf16[64,40]{1,0:T(8,128)(2,1)} %constant.14.clone.along_x) | copy-start | bytes 15364
  5.0 1.3 %collective-permute-start = (f32[80,128]{1,0:T(8,128)S(1)}, f32[80,128]{1,0:T(8,128)S(1)}, u32[]{:S(2)}, u32[]{:S(2)}) collective-permute-start(f32[80,128]{1,0:T(8,128)S(1)} %get-tuple-element.11), channel_id=1, source_target_pairs={{0,1},{1,0},{2,3},{3,2},{4,5},{5,4},{6,7},{7,6},{8,9},{9,8},{10,11... | collective-permute-start | bytes 122888 | tf_op jit(solution)/shard_map/ppermute | solution.py:633

commit v5 on v4

--- a/solution.py
+++ b/solution.py
@@ -209,15 +209,11 @@
 
 
 def pack_kernel(
-    corners_ref, slots_ref, near_ref, fine_ref, brick, const,
-    table_ref, own_ref, other_ref, planes_ref, window_ref,
-    table, table_sem,
+    corners_ref, slots_ref, near_ref, fine_ref, brick, const, table_ref, other_ref, planes_ref, table, table_sem
 ):
     make_table(corners_ref, slots_ref, near_ref, table_ref)
     fetch = pltpu.make_async_copy(table_ref, table, table_sem)
     fetch.start()
-    own_ref[...] = jnp.zeros_like(own_ref)
-    other_ref[...] = jnp.zeros_like(other_ref)
     planes_ref[...] = jnp.zeros_like(planes_ref)
     fetch.wait()
     me = lax.axis_index("gx_1")
@@ -230,6 +226,15 @@
                 at = e * 8 + half * 3 + k
                 planes_ref[at : at + 1, :] = row[:, half * 128 : half * 128 + 128]
 
+    pack_rows(table, brick, const, other_ref, None, 1)
+
+
+def pack_own_kernel(table, brick, const, own_ref, window_ref):
+    pack_rows(table, brick, const, own_ref, window_ref, 0)
+
+
+def pack_rows(table, brick, const, out, window_ref, dz):
+    out[...] = jnp.zeros_like(out)
     my_c = lax.axis_index("gz")
     lane = lax.broadcasted_iota(i32, (1, 128), 1)
     sub3 = lax.broadcasted_iota(i32, (3, 1), 0)
@@ -352,43 +357,41 @@
             row = row + 0.75 * spread
         return flat, total + jnp.sum(row, axis=0, keepdims=True)
 
-    for dz in range(2):
-        out = other_ref if dz else own_ref
-        z_shift = 256 * (1 - 2 * my_c) if dz else 0
-        for dy in (-1, 0, 1):
-            for dx in (0, -1, 1):
-                place = table[ROW_ANCHOR, (dx + 1) * 6 + (dy + 1) * 2 + dz]
-                y0, z0 = place >> 8, place & 255
-                z_base = z0 - 1 + z_shift
-                near = place >= 0
-                if dy == 1:
-                    near &= y0 == 0
-                if dy == -1:
-                    near &= y0 == 24
-                if dz:
-                    near &= z0 == jnp.where(my_c == 0, 0, 248)
-
-                @pl.when(near)
-                def _(out=out, dz=dz, dx=dx, dy=dy, y0=y0, z0=z0, z_base=z_base):
-                    if dy and dx:
-                        out[38:39, :] += diagonal_row(0 if dx == -1 else 31, dy, z_base)
-                    elif dy:
-                        out[48:80, :] += beside_rows(dy, z_base)
-                    elif dx:
-                        x, at = (0, 44) if dx == -1 else (31, 40)
-                        flat, row = edge_rows(x, y0, z_base)
-                        out[at : at + 3, :] = 0.75 * flat
-                        out[at + 3 : at + 4, :] = row
-                    else:
-                        rows, flats = all_rows(y0, z_base)
-                        out[0:32, :] = rows
-                        for i, flat in enumerate(flats):
-                            out[32 + i : 33 + i, :] = 0.25 * flat
-                        if dz == 0:
-                            start = (y0 >> 3) * 16 + (z0 >> 7) * 8
-                            for n in range(96):
-                                tile = brick[pl.ds(pl.multiple_of(n * 64 + start, 8), 8), :]
-                                window_ref[n * 8 : n * 8 + 8, :] = tile
+    z_shift = 256 * (1 - 2 * my_c) if dz else 0
+    for dy in (-1, 0, 1):
+        for dx in (0, -1, 1):
+            place = table[ROW_ANCHOR, (dx + 1) * 6 + (dy + 1) * 2 + dz]
+            y0, z0 = place >> 8, place & 255
+            z_base = z0 - 1 + z_shift
+            near = place >= 0
+            if dy == 1:
+                near &= y0 == 0
+            if dy == -1:
+                near &= y0 == 24
+            if dz:
+                near &= z0 == jnp.where(my_c == 0, 0, 248)
+
+            @pl.when(near)
+            def _(out=out, dz=dz, dx=dx, dy=dy, y0=y0, z0=z0, z_base=z_base):
+                if dy and dx:
+                    out[38:39, :] += diagonal_row(0 if dx == -1 else 31, dy, z_base)
+                elif dy:
+                    out[48:80, :] += beside_rows(dy, z_base)
+                elif dx:
+                    x, at = (0, 44) if dx == -1 else (31, 40)
+                    flat, row = edge_rows(x, y0, z_base)
+                    out[at : at + 3, :] = 0.75 * flat
+                    out[at + 3 : at + 4, :] = row
+                else:
+                    rows, flats = all_rows(y0, z_base)
+                    out[0:32, :] = rows
+                    for i, flat in enumerate(flats):
+                        out[32 + i : 33 + i, :] = 0.25 * flat
+                    if dz == 0:
+                        start = (y0 >> 3) * 16 + (z0 >> 7) * 8
+                        for n in range(96):
+                            tile = brick[pl.ds(pl.multiple_of(n * 64 + start, 8), 8), :]
+                            window_ref[n * 8 : n * 8 + 8, :] = tile
 
 
 def split_slot(slot):
@@ -616,21 +619,25 @@
     tiles = coarse_field.reshape(3, 32, 4, 8, 2, 128).transpose(0, 1, 2, 4, 3, 5).reshape(6144, 128)
     pack_const, beside = map(jnp.asarray, pack_constants())
     beside = beside.astype(jnp.bfloat16)
-    table, own, other, planes, window = pl.pallas_call(
+    table, other, planes = pl.pallas_call(
         pack_kernel,
-        out_shape=(
-            shape(8, 128, dtype=i32),
-            shape(PACKED, 128),
-            shape(PACKED, 128),
-            shape(32, 128),
-            shape(768, 128),
-        ),
+        out_shape=(shape(8, 128, dtype=i32), shape(PACKED, 128), shape(32, 128)),
         in_specs=[vmem()] * 6,
-        out_specs=(vmem(),) * 5,
+        out_specs=(vmem(),) * 3,
         scratch_shapes=[pltpu.SMEM((8, 128), i32), pltpu.SemaphoreType.DMA(())],
-        name="pack", compiler_params=pltpu.CompilerParams(vmem_limit_bytes=24 << 20),
+        name="pack",
+        compiler_params=pltpu.CompilerParams(vmem_limit_bytes=24 << 20),
     )(corners.T, grid_slot[None, :], neighbors.T, fine, tiles, pack_const)
     other = lax.ppermute(other, "gz", [(0, 1), (1, 0)])
+    own, window = pl.pallas_call(
+        pack_own_kernel,
+        out_shape=(shape(PACKED, 128), shape(768, 128)),
+        in_specs=[smem(), vmem(), vmem()],
+        out_specs=(vmem(),) * 2,
+        name="pack_own",
+        compiler_params=pltpu.CompilerParams(vmem_limit_bytes=24 << 20),
+        cost_estimate=pl.CostEstimate(flops=1 << 24, bytes_accessed=1 << 20, transcendentals=0),
+    )(table, tiles, pack_const)
     payload = pl.pallas_call(
         join_kernel,
         out_shape=shape(PLANE, FIRST, 128),

time: 74.4 us -> 74.4 us (level)
  blocking collectives: 62.2 us -> 64 us
  Pallas kernels: 7.67 us -> 6.51 us
  waiting for transfers between devices: 1.21 us -> 0.22 us
    all_to_all x1, blocking collectives: 18.9 us -> 20.6 us  [on_device(): held = lax.all_to_all(payload, ('gx_0', 'gy'), 0, 0)]
    pallas_call x1, Pallas kernels: 2.29 us -> 1.11 us  [on_device(): pl.pallas_call(pack_kernel, out_shape=(shape(8, 128, dtype=i32), shape(PA...]
    ppermute x1, waiting for transfers between devices: 1.21 us -> 0.22 us  [on_device(): other = lax.ppermute(other, 'gz', [(0, 1), (1, 0)])]
    pallas_call x0 -> x1, Pallas kernels: none -> 0.91 us  [on_device(): pl.pallas_call(pack_own_kernel, out_shape=(shape(PACKED, 128), shape(768,...]
    pallas_call x1, Pallas kernels: 1.5 us -> 0.64 us  [on_device(): pl.pallas_call(place_kernel, out_shape=shape(96, 32, 256), in_specs=[smem...]
  transfers between devices with their start and end apart: 1 -> 1, of which waited for: 1 -> 1; matrix products, arithmetic and copies ran while one was open for 0% -> 0% of each run, Pallas kernels for 0% -> 1%
where the time goes in v5:
time: 74.4 us; the launch traced here: 73.6 us
  blocking collectives  64 us (86%)
  Pallas kernels  6.51 us (9%)
  local copies, waits for them, and re-layouts  2.03 us (3%)
  between operations  0.81 us (1%)
    all_to_all x1, blocking collectives, on_device(): held = lax.all_to_all(payload, ('gx_0', 'gy'), 0, 0)  20.6 us
    all_to_all x1, blocking collectives, on_device(): received = lax.all_to_all(routed, 'gx_1', 0, 0)  18.5 us
    all_to_all x1, blocking collectives, on_device(): held_means = lax.all_to_all(means, ('gx_0', 'gy'), 0, 0)  12.7 us
    all_to_all x1, blocking collectives, on_device(): returned = lax.all_to_all(back, 'gx_1', 0, 0)  12.2 us
    unnamed x25, local copies, waits for them, and re-layouts  2.03 us
    pallas_call x1, Pallas kernels, on_device(): pl.pallas_call(update_kernel, out_shape=(shape(3 * SLOTS * F, F * F), sha...  1.88 us
  transfers between devices with their start and end apart: 1, of which 1 were waited for; matrix products, arithmetic and copies ran while one was open for 0% of the time, Pallas kernels for 1%

profile of v5, /device:TPU:2, one launch (start us, length us, event | category | flops | bytes accessed | tf_op | source)
XLA Modules:
  0.0 73.6 jit_solution(6264016654755616173)
XLA Ops:
  0.6 0.0 copy-start.4
  0.6 0.0 copy-start.1
  0.7 0.0 copy-start.9
  0.7 0.0 copy-start.11
  0.7 0.0 copy-start.10
  0.7 2.0 %copy.17 = f32[3,32,32,256]{3,2,1,0:T(8,128)S(1)} copy(f32[3,32,32,256]{3,2,1,0:T(8,128)} %param.12) | data formatting | bytes 6291456
  2.6 0.0 copy-start
  2.6 0.0 copy-done.4
  2.6 0.0 copy-done.1
  2.6 0.0 copy-done.9
  2.7 0.0 copy-done.11
  2.7 0.0 copy-done.10
  2.7 1.1 %pack.1 = (s32[8,128]{1,0:T(8,128)S(1)}, f32[80,128]{1,0:T(8,128)S(1)}, f32[32,128]{1,0:T(8,128)S(1)}) custom-call(s32[3,512]{1,0:T(4,128)S(1)} %bitcast.20, s32[1,512]{1,0:T(1,128)S(1)} %bitcast.22, s32[2,512]{1,0:T(2,128)S(1)} %bitcast.21, f32[192,256]{1,0:T(8,128)S(1)} %bitcast.17, f32[6144,128]{1,0:T(8,128)S(1)} %bitcast.13, f32[40,128]{1,0:T(8,128)S(1)} %copy-done.4), custom_call_target="tpu_custom_call" | custom-call | tf_op jit(solution)/shard_map/pack/pallas_call | solution.py:622
  3.8 0.0 copy-start.7
  3.8 0.1 collective-permute-start
  3.9 0.0 copy-start.2
  3.9 0.0 copy-start.3
  3.9 0.0 copy-start.5
  3.9 0.0 copy-start.6
  4.0 0.0 copy-start.8
  4.0 0.9 %pack_own.1 = (f32[80,128]{1,0:T(8,128)S(1)}, f32[768,128]{1,0:T(8,128)S(1)}) custom-call(s32[8,128]{1,0:T(8,128)S(1)} %get-tuple-element.9.table, f32[6144,128]{1,0:T(8,128)S(1)} %bitcast.14, f32[40,128]{1,0:T(8,128)S(1)} %copy-done.4), custom_call_target="tpu_custom_call" | custom-call | flops 16777216 | bytes 1048576 | tf_op jit(solution)/shard_map/pack_own/pallas_call | solution.py:632
  4.9 0.0 copy-done
  4.9 0.2 collective-permute-done.other
  5.1 0.1 join.1
  5.2 20.6 %all_to_all.20.held = f32[16,88,128]{2,1,0:T(8,128)S(1)} all-to-all(f32[16,88,128]{2,1,0:T(8,128)S(1)} %join.1), channel_id=1, replica_groups=mesh['gx_0'=4,'gx_1'=8,'gy'=4,'gz'=2] {'gx_0','gy'}, dimensions={0} | all-to-all | bytes 1441792 | tf_op jit(solution)/shard_map/all_to_all | solution.py:649
  25.8 0.0 copy-done.7
  25.8 1.1 %route.1 = f32[8,56,128]{2,1,0:T(8,128)S(1)} custom-call(s32[8,128]{1,0:T(8,128)S(1)} %get-tuple-element.9.table, f32[16,88,128]{2,1,0:T(8,128)S(1)} %all_to_all.20.held, bf16[128,128]{1,0:T(8,128)(2,1)S(1)} %copy-done.7), custom_call_target="tpu_custom_call" | custom-call | tf_op jit(solution)/shard_map/route/pallas_call | solution.py:650
  26.8 18.5 %all_to_all.21.rcv = f32[8,56,128]{2,1,0:T(8,128)S(1)} all-to-all(f32[8,56,128]{2,1,0:T(8,128)S(1)} %route.1), channel_id=1, replica_groups=mesh['gx_0'=4,'gx_1'=8,'gy'=4,'gz'=2] {'gx_1'}, dimensions={0} | all-to-all | bytes 458752 | tf_op jit(solution)/shard_map/all_to_all | solution.py:659
  45.4 0.0 copy-done.2
  45.4 0.0 copy-done.3
  45.4 0.0 copy-done.5
  45.4 0.0 copy-done.6
  45.4 0.0 copy-done.8
  45.4 1.9 %update.1 = (f32[192,256]{1,0:T(8,128)}, f32[16,48,128]{2,1,0:T(8,128)S(1)}) custom-call(s32[8,128]{1,0:T(8,128)S(1)} %get-tuple-element.9.table, f32[8,56,128]{2,1,0:T(8,128)S(1)} %all_to_all.21.rcv, f32[192,256]{1,0:T(8,128)S(1)} %bitcast.18, f32[64,256]{1,0:T(8,128)S(1)} %bitcast.19, bf16[64,40]{1,0:T(8,128)(2,1)S(1)} %copy-done.8, ...), custom_call_target="tpu_custom_call" | custom-call | tf_op jit(solution)/shard_map/update/pallas_call | solution.py:660
  47.3 12.7 %all_to_all.22.held = f32[16,48,128]{2,1,0:T(8,128)S(1)} all-to-all(f32[16,48,128]{2,1,0:T(8,128)S(1)} %get-tuple-element.14), channel_id=1, replica_groups=mesh['gx_0'=4,'gx_1'=8,'gy'=4,'gz'=2] {'gx_0','gy'}, dimensions={0} | all-to-all | bytes 786432 | tf_op jit(solution)/shard_map/all_to_all | solution.py:675
  60.0 0.8 %send_back.1 = f32[8,48,128]{2,1,0:T(8,128)S(1)} custom-call(s32[8,128]{1,0:T(8,128)S(1)} %get-tuple-element.9.table, f32[16,48,128]{2,1,0:T(8,128)S(1)} %all_to_all.22.held), custom_call_target="tpu_custom_call" | custom-call | tf_op jit(solution)/shard_map/send_back/pallas_call | solution.py:676
  60.8 12.2 %all_to_all.23.rcv = f32[8,48,128]{2,1,0:T(8,128)S(1)} all-to-all(f32[8,48,128]{2,1,0:T(8,128)S(1)} %send_back.1), channel_id=1, replica_groups=mesh['gx_0'=4,'gx_1'=8,'gy'=4,'gz'=2] {'gx_1'}, dimensions={0} | all-to-all | bytes 393216 | tf_op jit(solution)/shard_map/all_to_all | solution.py:683
  73.0 0.6 place.1
Async XLA Ops:
  0.6 2.0 %copy-start.4 = (f32[40,128]{1,0:T(8,128)S(1)}, f32[40,128]{1,0:T(8,128)}, u32[]{:S(2)}) copy-start(f32[40,128]{1,0:T(8,128)} %constant.12.clone.const) | copy-start | bytes 61444
  0.6 2.0 %copy-start.1 = (f32[3,4,16,256]{3,2,1,0:T(8,128)S(1)}, f32[3,4,16,256]{3,2,1,0:T(8,128)}, u32[]{:S(2)}) copy-start(f32[3,4,16,256]{3,2,1,0:T(8,128)} %param.13) | copy-start | bytes 589828
  0.7 2.0 %copy-start.9 = (s32[512,3]{0,1:T(4,128)S(1)}, s32[512,3]{0,1:T(4,128)}, u32[]{:S(2)}) copy-start(s32[512,3]{0,1:T(4,128)} %param.15) | copy-start | bytes 18436
  0.7 2.0 %copy-start.11 = (s32[512]{0:T(512)S(1)}, s32[512]{0:T(512)}, u32[]{:S(2)}) copy-start(s32[512]{0:T(512)} %param.16) | copy-start | bytes 6148
  0.7 2.0 %copy-start.10 = (s32[512,2]{0,1:T(2,128)S(1)}, s32[512,2]{0,1:T(2,128)}, u32[]{:S(2)}) copy-start(s32[512,2]{0,1:T(2,128)} %param.17) | copy-start | bytes 12292
  2.6 2.2 %copy-start = (f32[3,32,32,256]{3,2,1,0:T(8,128)}, f32[3,32,32,256]{3,2,1,0:T(8,128)S(1)}, u32[]{:S(2)}) copy-start(f32[3,32,32,256]{3,2,1,0:T(8,128)S(1)} %copy.17) | copy-start | bytes 9437188
  3.8 22.0 %copy-start.7 = (bf16[128,128]{1,0:T(8,128)(2,1)S(1)}, bf16[128,128]{1,0:T(8,128)(2,1)}, u32[]{:S(2)}) copy-start(bf16[128,128]{1,0:T(8,128)(2,1)} %constant.20.beside_ref) | copy-start | bytes 98308
  3.8 1.3 %collective-permute-start = (f32[80,128]{1,0:T(8,128)S(1)}, f32[80,128]{1,0:T(8,128)S(1)}, u32[]{:S(2)}, u32[]{:S(2)}) collective-permute-start(f32[80,128]{1,0:T(8,128)S(1)} %get-tuple-element.11), channel_id=1, source_target_pairs={{0,1},{1,0},{2,3},{3,2},{4,5},{5,4},{6,7},{7,6},{8,9},{9,8},{10,11... | collective-permute-start | bytes 122888 | tf_op jit(solution)/shard_map/ppermute | solution.py:631
  3.9 41.5 %copy-start.2 = (bf16[128,768]{1,0:T(8,128)(2,1)S(1)}, bf16[128,768]{1,0:T(8,128)(2,1)}, u32[]{:S(2)}) copy-start(bf16[128,768]{1,0:T(8,128)(2,1)} %constant.15.clone.faces) | copy-start | bytes 589828
  3.9 41.5 %copy-start.3 = (bf16[2,256,128]{2,1,0:T(8,128)(2,1)S(1)}, bf16[2,256,128]{2,1,0:T(8,128)(2,1)}, u32[]{:S(2)}) copy-start(bf16[2,256,128]{2,1,0:T(8,128)(2,1)} %constant.17.clone.pool) | copy-start | bytes 393220
  3.9 41.4 %copy-start.5 = (f32[4,16,256]{2,1,0:T(8,128)S(1)}, f32[4,16,256]{2,1,0:T(8,128)}, u32[]{:S(2)}) copy-start(f32[4,16,256]{2,1,0:T(8,128)} %param.14) | copy-start | bytes 196612
  3.9 41.4 %copy-start.6 = (bf16[128,256]{1,0:T(8,128)(2,1)S(1)}, bf16[128,256]{1,0:T(8,128)(2,1)}, u32[]{:S(2)}) copy-start(bf16[128,256]{1,0:T(8,128)(2,1)} %constant.16.clone.ends) | copy-start | bytes 196612
  4.0 41.4 %copy-start.8 = (bf16[64,40]{1,0:T(8,128)(2,1)S(1)}, bf16[64,40]{1,0:T(8,128)(2,1)}, u32[]{:S(2)}) copy-start(bf16[64,40]{1,0:T(8,128)(2,1)} %constant.14.clone.along_x) | copy-start | bytes 15364

commit v6 on v5

--- a/solution.py
+++ b/solution.py
@@ -103,14 +103,14 @@
     return high, middle, (rest - middle.astype(f32)).astype(jnp.bfloat16)
 
 
-def dot_right(values, weights):
-    parts = [jnp.dot(part, weights, preferred_element_type=f32) for part in thirds(values)]
-    return parts[0] + (parts[1] + parts[2])
+def dot_right(values, weights, pieces=2):
+    parts = [jnp.dot(part, weights, preferred_element_type=f32) for part in thirds(values)[:pieces]]
+    return sum(parts[1:], parts[0])
 
 
 def dot_left(weights, values):
-    parts = [jnp.dot(weights, part, preferred_element_type=f32) for part in thirds(values)]
-    return parts[0] + (parts[1] + parts[2])
+    parts = [jnp.dot(weights, part, preferred_element_type=f32) for part in thirds(values)[:2]]
+    return sum(parts[1:], parts[0])
 
 
 def position():
@@ -541,8 +541,8 @@
     store.start()
     for p in range(2):
         at = p * 96
-        pooled[p * 48 : p * 48 + 48, :] = dot_right(advanced[at : at + 48, :], pool[0]) + dot_right(
-            advanced[at + 48 : at + 96, :], pool[1]
+        pooled[p * 48 : p * 48 + 48, :] = dot_right(advanced[at : at + 48, :], pool[0], 3) + dot_right(
+            advanced[at + 48 : at + 96, :], pool[1], 3
         )
     means = pooled[pl.ds(0, 48, stride=2), :] + pooled[pl.ds(1, 48, stride=2), :]
     for j in range(PLANE):

time: 74.4 us -> 74.2 us (level)
  transfers between devices with their start and end apart: 1 -> 1, of which waited for: 1 -> 0; matrix products, arithmetic and copies ran while one was open for 0% -> 0% of each run, Pallas kernels for 1% -> 2%
where the time goes in v6:
time: 74.2 us; the launch traced here: 73.5 us
  blocking collectives  63.8 us (86%)
  Pallas kernels  6.7 us (9%)
  local copies, waits for them, and re-layouts  2.01 us (3%)
  between operations  0.76 us (1%)
    all_to_all x1, blocking collectives, on_device(): held = lax.all_to_all(payload, ('gx_0', 'gy'), 0, 0)  19.9 us
    all_to_all x1, blocking collectives, on_device(): received = lax.all_to_all(routed, 'gx_1', 0, 0)  19.2 us
    all_to_all x1, blocking collectives, on_device(): held_means = lax.all_to_all(means, ('gx_0', 'gy'), 0, 0)  12.5 us
    all_to_all x1, blocking collectives, on_device(): returned = lax.all_to_all(back, 'gx_1', 0, 0)  12.2 us
    unnamed x25, local copies, waits for them, and re-layouts  2.01 us
    pallas_call x1, Pallas kernels, on_device(): pl.pallas_call(update_kernel, out_shape=(shape(3 * SLOTS * F, F * F), sha...  1.82 us
  transfers between devices with their start and end apart: 1, of which 0 were waited for; matrix products, arithmetic and copies ran while one was open for 0% of the time, Pallas kernels for 2%

profile of v6, /device:TPU:2, one launch (start us, length us, event | category | flops | bytes accessed | tf_op | source)
XLA Modules:
  0.0 73.5 jit_solution(5703441173285653256)
XLA Ops:
  0.6 0.0 copy-start.4
  0.6 0.0 copy-start.1
  0.7 0.0 copy-start.9
  0.7 0.0 copy-start.11
  0.7 0.0 copy-start.10
  0.7 2.0 %copy.17 = f32[3,32,32,256]{3,2,1,0:T(8,128)S(1)} copy(f32[3,32,32,256]{3,2,1,0:T(8,128)} %param.12) | data formatting | bytes 6291456
  2.6 0.0 copy-start
  2.6 0.0 copy-done.4
  2.6 0.0 copy-done.1
  2.6 0.0 copy-done.9
  2.7 0.0 copy-done.11
  2.7 0.0 copy-done.10
  2.7 1.1 %pack.1 = (s32[8,128]{1,0:T(8,128)S(1)}, f32[80,128]{1,0:T(8,128)S(1)}, f32[32,128]{1,0:T(8,128)S(1)}) custom-call(s32[3,512]{1,0:T(4,128)S(1)} %bitcast.20, s32[1,512]{1,0:T(1,128)S(1)} %bitcast.22, s32[2,512]{1,0:T(2,128)S(1)} %bitcast.21, f32[192,256]{1,0:T(8,128)S(1)} %bitcast.17, f32[6144,128]{1,0:T(8,128)S(1)} %bitcast.13, f32[40,128]{1,0:T(8,128)S(1)} %copy-done.4), custom_call_target="tpu_custom_call" | custom-call | tf_op jit(solution)/shard_map/pack/pallas_call | solution.py:622
  3.8 0.0 copy-start.7
  3.8 0.2 collective-permute-start
  4.0 0.0 copy-start.2
  4.0 0.0 copy-start.3
  4.0 0.0 copy-start.5
  4.0 0.0 copy-start.6
  4.0 0.0 copy-start.8
  4.1 1.2 %pack_own.1 = (f32[80,128]{1,0:T(8,128)S(1)}, f32[768,128]{1,0:T(8,128)S(1)}) custom-call(s32[8,128]{1,0:T(8,128)S(1)} %get-tuple-element.9.table, f32[6144,128]{1,0:T(8,128)S(1)} %bitcast.14, f32[40,128]{1,0:T(8,128)S(1)} %copy-done.4), custom_call_target="tpu_custom_call" | custom-call | flops 16777216 | bytes 1048576 | tf_op jit(solution)/shard_map/pack_own/pallas_call | solution.py:632
  5.3 0.0 copy-done
  5.3 0.0 collective-permute-done.other
  5.3 0.1 join.1
  5.3 19.9 %all_to_all.20.held = f32[16,88,128]{2,1,0:T(8,128)S(1)} all-to-all(f32[16,88,128]{2,1,0:T(8,128)S(1)} %join.1), channel_id=1, replica_groups=mesh['gx_0'=4,'gx_1'=8,'gy'=4,'gz'=2] {'gx_0','gy'}, dimensions={0} | all-to-all | bytes 1441792 | tf_op jit(solution)/shard_map/all_to_all | solution.py:649
  25.2 0.0 copy-done.7
  25.2 1.0 %route.1 = f32[8,56,128]{2,1,0:T(8,128)S(1)} custom-call(s32[8,128]{1,0:T(8,128)S(1)} %get-tuple-element.9.table, f32[16,88,128]{2,1,0:T(8,128)S(1)} %all_to_all.20.held, bf16[128,128]{1,0:T(8,128)(2,1)S(1)} %copy-done.7), custom_call_target="tpu_custom_call" | custom-call | tf_op jit(solution)/shard_map/route/pallas_call | solution.py:650
  26.2 19.2 %all_to_all.21.rcv = f32[8,56,128]{2,1,0:T(8,128)S(1)} all-to-all(f32[8,56,128]{2,1,0:T(8,128)S(1)} %route.1), channel_id=1, replica_groups=mesh['gx_0'=4,'gx_1'=8,'gy'=4,'gz'=2] {'gx_1'}, dimensions={0} | all-to-all | bytes 458752 | tf_op jit(solution)/shard_map/all_to_all | solution.py:659
  45.5 0.0 copy-done.2
  45.5 0.0 copy-done.3
  45.5 0.0 copy-done.5
  45.5 0.0 copy-done.6
  45.5 0.0 copy-done.8
  45.5 1.8 %update.1 = (f32[192,256]{1,0:T(8,128)}, f32[16,48,128]{2,1,0:T(8,128)S(1)}) custom-call(s32[8,128]{1,0:T(8,128)S(1)} %get-tuple-element.9.table, f32[8,56,128]{2,1,0:T(8,128)S(1)} %all_to_all.21.rcv, f32[192,256]{1,0:T(8,128)S(1)} %bitcast.18, f32[64,256]{1,0:T(8,128)S(1)} %bitcast.19, bf16[64,40]{1,0:T(8,128)(2,1)S(1)} %copy-done.8, ...), custom_call_target="tpu_custom_call" | custom-call | tf_op jit(solution)/shard_map/update/pallas_call | solution.py:660
  47.3 12.5 %all_to_all.22.held = f32[16,48,128]{2,1,0:T(8,128)S(1)} all-to-all(f32[16,48,128]{2,1,0:T(8,128)S(1)} %get-tuple-element.14), channel_id=1, replica_groups=mesh['gx_0'=4,'gx_1'=8,'gy'=4,'gz'=2] {'gx_0','gy'}, dimensions={0} | all-to-all | bytes 786432 | tf_op jit(solution)/shard_map/all_to_all | solution.py:675
  59.8 0.8 %send_back.1 = f32[8,48,128]{2,1,0:T(8,128)S(1)} custom-call(s32[8,128]{1,0:T(8,128)S(1)} %get-tuple-element.9.table, f32[16,48,128]{2,1,0:T(8,128)S(1)} %all_to_all.22.held), custom_call_target="tpu_custom_call" | custom-call | tf_op jit(solution)/shard_map/send_back/pallas_call | solution.py:676
  60.7 12.2 %all_to_all.23.rcv = f32[8,48,128]{2,1,0:T(8,128)S(1)} all-to-all(f32[8,48,128]{2,1,0:T(8,128)S(1)} %send_back.1), channel_id=1, replica_groups=mesh['gx_0'=4,'gx_1'=8,'gy'=4,'gz'=2] {'gx_1'}, dimensions={0} | all-to-all | bytes 393216 | tf_op jit(solution)/shard_map/all_to_all | solution.py:683
  72.8 0.6 place.1
Async XLA Ops:
  0.6 2.0 %copy-start.4 = (f32[40,128]{1,0:T(8,128)S(1)}, f32[40,128]{1,0:T(8,128)}, u32[]{:S(2)}) copy-start(f32[40,128]{1,0:T(8,128)} %constant.12.clone.const) | copy-start | bytes 61444
  0.6 2.0 %copy-start.1 = (f32[3,4,16,256]{3,2,1,0:T(8,128)S(1)}, f32[3,4,16,256]{3,2,1,0:T(8,128)}, u32[]{:S(2)}) copy-start(f32[3,4,16,256]{3,2,1,0:T(8,128)} %param.13) | copy-start | bytes 589828
  0.7 2.0 %copy-start.9 = (s32[512,3]{0,1:T(4,128)S(1)}, s32[512,3]{0,1:T(4,128)}, u32[]{:S(2)}) copy-start(s32[512,3]{0,1:T(4,128)} %param.15) | copy-start | bytes 18436
  0.7 2.0 %copy-start.11 = (s32[512]{0:T(512)S(1)}, s32[512]{0:T(512)}, u32[]{:S(2)}) copy-start(s32[512]{0:T(512)} %param.16) | copy-start | bytes 6148
  0.7 2.0 %copy-start.10 = (s32[512,2]{0,1:T(2,128)S(1)}, s32[512,2]{0,1:T(2,128)}, u32[]{:S(2)}) copy-start(s32[512,2]{0,1:T(2,128)} %param.17) | copy-start | bytes 12292
  2.6 2.6 %copy-start = (f32[3,32,32,256]{3,2,1,0:T(8,128)}, f32[3,32,32,256]{3,2,1,0:T(8,128)S(1)}, u32[]{:S(2)}) copy-start(f32[3,32,32,256]{3,2,1,0:T(8,128)S(1)} %copy.17) | copy-start | bytes 9437188
  3.8 21.4 %copy-start.7 = (bf16[128,128]{1,0:T(8,128)(2,1)S(1)}, bf16[128,128]{1,0:T(8,128)(2,1)}, u32[]{:S(2)}) copy-start(bf16[128,128]{1,0:T(8,128)(2,1)} %constant.20.beside_ref) | copy-start | bytes 98308
  3.8 1.5 %collective-permute-start = (f32[80,128]{1,0:T(8,128)S(1)}, f32[80,128]{1,0:T(8,128)S(1)}, u32[]{:S(2)}, u32[]{:S(2)}) collective-permute-start(f32[80,128]{1,0:T(8,128)S(1)} %get-tuple-element.11), channel_id=1, source_target_pairs={{0,1},{1,0},{2,3},{3,2},{4,5},{5,4},{6,7},{7,6},{8,9},{9,8},{10,11... | collective-permute-start | bytes 122888 | tf_op jit(solution)/shard_map/ppermute | solution.py:631
  4.0 41.4 %copy-start.2 = (bf16[128,768]{1,0:T(8,128)(2,1)S(1)}, bf16[128,768]{1,0:T(8,128)(2,1)}, u32[]{:S(2)}) copy-start(bf16[128,768]{1,0:T(8,128)(2,1)} %constant.15.clone.faces) | copy-start | bytes 589828
  4.0 41.4 %copy-start.3 = (bf16[2,256,128]{2,1,0:T(8,128)(2,1)S(1)}, bf16[2,256,128]{2,1,0:T(8,128)(2,1)}, u32[]{:S(2)}) copy-start(bf16[2,256,128]{2,1,0:T(8,128)(2,1)} %constant.17.clone.pool) | copy-start | bytes 393220
  4.0 41.4 %copy-start.5 = (f32[4,16,256]{2,1,0:T(8,128)S(1)}, f32[4,16,256]{2,1,0:T(8,128)}, u32[]{:S(2)}) copy-start(f32[4,16,256]{2,1,0:T(8,128)} %param.14) | copy-start | bytes 196612
  4.0 41.4 %copy-start.6 = (bf16[128,256]{1,0:T(8,128)(2,1)S(1)}, bf16[128,256]{1,0:T(8,128)(2,1)}, u32[]{:S(2)}) copy-start(bf16[128,256]{1,0:T(8,128)(2,1)} %constant.16.clone.ends) | copy-start | bytes 196612
  4.0 41.4 %copy-start.8 = (bf16[64,40]{1,0:T(8,128)(2,1)S(1)}, bf16[64,40]{1,0:T(8,128)(2,1)}, u32[]{:S(2)}) copy-start(bf16[64,40]{1,0:T(8,128)(2,1)} %constant.14.clone.along_x) | copy-start | bytes 15364
